TPU v7x, 256 devices: a whole 4x4x8 slice. The times are simulated.
256 devices in a mesh: row: 16 (over x, y), col: 16 (over z, core).
Axes of the slice: x: 4, y: 4, z: 8, core: 2. Of those that a mesh axis runs over, the one named last changes fastest.
Arguments:
- inputs: bfloat16 [2048, 16384], P('col', 'row'), may hold values from -6 to 6
- weight: bfloat16 [16384, 16384], P('row', 'col'), may hold values from -0.046875 to 0.046875
- cotangent: bfloat16 [2048, 16384], P('row', 'col'), may hold values from -0.75 to 0.75
- scale_in: float32 [8, 16384], P(None, 'row'), may hold values from -4 to 4
- scale_out: float32 [8, 16384], P(None, 'col'), may hold values from -4 to 4
- member: int32 [2048], replicated, may hold values from 0 to 7
Outputs:
- input_grad: bfloat16 [2048, 16384], P('col', 'row')
- weight_grad: float32 [16384, 16384], P('row', 'col')
- in_factor_grad: float32 [8, 16384], P(None, 'row')
- out_factor_grad: float32 [8, 16384], P(None, 'col')
All inputs are finite; a program needn't handle non-finite values.
Results may differ from a plain program's by a relative error of at most 0.0049.
Values may be sent and summed in bfloat16 or wider, within the bound.
A program may use at most 128 MiB of HBM per device.

v0:
```python
import jax
import jax.numpy as jnp
from jax import lax
from jax.sharding import PartitionSpec as P

highest = lax.Precision.HIGHEST


def from_everyone(value, axis):
    copies = jnp.broadcast_to(value, (lax.axis_size(axis), *value.shape))
    return lax.all_to_all(copies, axis, split_axis=0, concat_axis=0, tiled=True)


def of_everyone(value, axis):
    return from_everyone(value, axis).sum(axis=0)


def gathered_total(value, axis):
    return lax.all_gather(value, axis).sum(0)


def member_sums(one_hot, values):
    return jnp.dot(one_hot.T, values, precision=highest)


def local(inputs, weight, cotangent, scale_in, scale_out, member):
    n_members = scale_in.shape[0]
    one_hot = (member[:, None] == jnp.arange(n_members, dtype=jnp.int32)[None, :]).astype(
        jnp.float32
    )
    full_inputs = lax.all_gather(inputs, "col", axis=0, tiled=True)
    full_cot = lax.all_gather(cotangent, "row", axis=0, tiled=True)
    r_rows = jnp.dot(one_hot, scale_in, precision=highest)
    s_rows = jnp.dot(one_hot, scale_out, precision=highest)
    scaled_in = (full_inputs * r_rows).astype(jnp.bfloat16)
    scaled_cot = (full_cot * s_rows).astype(jnp.bfloat16)
    batch = scaled_in.shape[0]
    pre_part = jnp.dot(scaled_in, weight, preferred_element_type=jnp.float32)
    out_term = member_sums(one_hot, full_cot.astype(jnp.float32) * pre_part)
    out_factor_grad = of_everyone(out_term, "row")
    col_share = batch // lax.axis_size("col")
    col_start = lax.axis_index("col") * col_share
    back_part = lax.dot_general(
        scaled_cot, weight, (((1,), (1,)), ((), ())), preferred_element_type=jnp.float32
    )
    in_term = member_sums(one_hot, full_inputs.astype(jnp.float32) * back_part)
    in_factor_grad = gathered_total(in_term, "col")
    back_block = lax.psum_scatter(back_part, "col", scatter_dimension=0, tiled=True)
    r_block = lax.dynamic_slice_in_dim(r_rows, col_start, col_share, 0)
    input_grad = (back_block * r_block).astype(jnp.bfloat16)
    weight_grad = lax.dot_general(
        scaled_in, scaled_cot, (((0,), (0,)), ((), ())), preferred_element_type=jnp.float32
    )
    return (input_grad, weight_grad, in_factor_grad, out_factor_grad)


def solution(mesh):
    placed = (
        P("col", "row"),
        P("row", "col"),
        P("row", "col"),
        P(None, "row"),
        P(None, "col"),
        P(),
    )
    return jax.shard_map(
        local,
        mesh=mesh,
        in_specs=placed,
        out_specs=(P("col", "row"), P("row", "col"), P(None, "row"), P(None, "col")),
        check_vma=False,
    )
```

profile of v0, /device:TPU:1, one launch (start us, length us, event | category | flops | bytes accessed | tf_op | source)
XLA Modules:
  0.0 193.9 jit_solution(3907940686163401925)
XLA Ops:
  7.2 0.0 copy-start
  7.2 0.0 all-gather.4.cloned.1.call-start
  7.2 0.7 all-gather.4.cloned.1.call-update
  7.9 0.0 all-gather.6.cloned.1.call-start
  8.0 0.7 all-gather.6.cloned.1.call-update
  8.7 0.0 reduce-scatter.2.cloned.1.call-start
  8.7 61.8 %all-gather.4.cloned.1.call-done = bf16[2048,1024]{1,0:T(8,128)(2,1)} async-done(((bf16[128,1024]{1,0:T(8,128)(2,1)}), bf16[2048,1024]{1,0:T(8,128)(2,1)}) %all-gather.4.cloned.1.call-update) | async-done | bytes 4194320 | tf_op jit(solution)/shard_map/all_gather | solution.py:32
  70.5 5.6 %fusion = bf16[2048,1024]{1,0:T(8,128)(2,1)S(1)} fusion(bf16[2048,1024]{1,0:T(8,128)(2,1)} %all-gather.4.cloned.1.call-done, f32[8,1024]{1,0:T(8,128)} %param.10, s32[2048]{0:T(1024)} %param.11), kind=kOutput, calls=%fused_computation.4 | convolution fusion | flops 207634432 | bytes 8429568 | tf_op jit(solution)/shard_map/dot_general | solution.py:34
  76.1 0.0 copy-start.2
  76.1 2.0 %copy-done.2 = bf16[2048,1024]{1,0:T(8,128)(2,1)} copy-done((bf16[2048,1024]{1,0:T(8,128)(2,1)}, bf16[2048,1024]{1,0:T(8,128)(2,1)S(1)}, u32[]{:S(2)}) %copy-start.2) | copy-done | bytes 4194328
  78.1 0.0 copy-done
  78.1 7.1 %fusion.13 = f32[2048,1024]{1,0:T(8,128)} fusion(bf16[2048,1024]{1,0:T(8,128)(2,1)S(1)} %fusion, bf16[1024,1024]{1,0:T(8,128)(2,1)S(1)} %copy-done), kind=kOutput, calls=%fused_computation.18 | convolution fusion | flops 4294967296 | bytes 14680064 | tf_op jit(solution)/shard_map/dot_general | solution.py:43
  85.1 0.0 copy-start.4
  85.1 0.0 copy-start.5
  85.1 0.0 reduce-scatter.2.cloned.1.call-update
  85.1 0.7 copy-done.4
  85.8 0.1 copy-done.5
  85.9 5.6 %fusion.4 = f32[2048,1024]{1,0:T(8,128)} fusion(f32[8,1024]{1,0:T(8,128)S(1)} %copy-done.5, s32[2048]{0:T(1024)S(1)} %copy-done.4), kind=kOutput, calls=%fused_computation.9 | convolution fusion | flops 201342976 | bytes 8429568 | tf_op jit(solution)/shard_map/dot_general | solution.py:33
  91.5 23.0 %all-gather.6.cloned.1.call-done = bf16[2048,1024]{1,0:T(8,128)(2,1)} async-done(((bf16[128,1024]{1,0:T(8,128)(2,1)}), bf16[2048,1024]{1,0:T(8,128)(2,1)}) %all-gather.6.cloned.1.call-update) | async-done | bytes 4194320 | tf_op jit(solution)/shard_map/all_gather | solution.py:31
  114.5 0.0 copy-start.1
  114.5 7.7 %fusion.9 = f32[2048,1024]{1,0:T(8,128)S(1)} fusion(bf16[1024,1024]{1,0:T(8,128)(2,1)S(1)} %copy-done, f32[2048,1024]{1,0:T(8,128)} %fusion.4, bf16[2048,1024]{1,0:T(8,128)(2,1)} %all-gather.6.cloned.1.call-done), kind=kOutput, calls=%fused_computation.16 | convolution fusion | flops 4301258752 | bytes 23068672 | tf_op jit(solution)/shard_map/dot_general | solution.py:38
  122.2 0.0 copy-done.1
  122.3 3.4 %fusion.1 = f32[8,1024]{1,0:T(8,128)S(1)} fusion(f32[2048,1024]{1,0:T(8,128)S(1)} %fusion.9, bf16[2048,1024]{1,0:T(8,128)(2,1)S(1)} %copy-done.1, s32[2048]{0:T(1024)S(1)} %copy-done.4), kind=kOutput, calls=%fused_computation.5 | convolution fusion | flops 205537280 | bytes 12623872 | tf_op jit(solution)/shard_map/dot_general | solution.py:23
  125.7 0.9 broadcast_in_dim.2
  126.6 6.5 %all-to-all-start = ((f32[16,8,1024]{2,1,0:T(8,128)}), f32[16,8,1024]{2,1,0:T(8,128)S(1)}, u32[]{:S(2)}, u32[]{:S(2)}) async-start(f32[16,8,1024]{2,1,0:T(8,128)} %broadcast_in_dim.2), calls=%async_computation.1 | async-start | bytes 1048576 | tf_op jit(solution)/shard_map/all_to_all | solution.py:11
  133.1 0.0 copy-start.3
  133.1 13.0 %fusion.11 = f32[1024,1024]{1,0:T(8,128)} fusion(bf16[2048,1024]{1,0:T(8,128)(2,1)} %copy-done.2, f32[2048,1024]{1,0:T(8,128)} %fusion.4, bf16[2048,1024]{1,0:T(8,128)(2,1)} %all-gather.6.cloned.1.call-done), kind=kOutput, calls=%fused_computation.17 | convolution fusion | flops 4301258752 | bytes 20971520 | tf_op jit(solution)/shard_map/dot_general | solution.py:51
  146.1 0.0 copy-done.3
  146.1 5.8 %fusion.3 = f32[8,1024]{1,0:T(8,128)S(1)} fusion(f32[2048,1024]{1,0:T(8,128)} %fusion.13, bf16[2048,1024]{1,0:T(8,128)(2,1)S(1)} %copy-done.3, s32[2048]{0:T(1024)S(1)} %copy-done.4), kind=kOutput, calls=%fused_computation.7 | convolution fusion | flops 205537280 | bytes 12623872 | tf_op jit(solution)/shard_map/dot_general | solution.py:23
  151.9 18.7 %all-gather = f32[128,1024]{1,0:T(8,128)S(1)} all-gather(f32[8,1024]{1,0:T(8,128)S(1)} %fusion.3), channel_id=2, replica_groups=mesh['row'=16,'col'=16] {'col'}, dimensions={0}, use_global_device_ids=true | all-gather | bytes 557056 | tf_op jit(solution)/shard_map/all_gather | solution.py:19
  170.6 0.6 bitcast_reduce_fusion
  171.3 0.0 all-to-all-done
  171.3 0.6 reduce_sum.19
  171.9 13.6 %reduce-scatter.2.cloned.1.call-done = f32[128,1024]{1,0:T(8,128)} async-done(((f32[2048,1024]{1,0:T(8,128)}), f32[128,1024]{1,0:T(8,128)}) %reduce-scatter.2.cloned.1.call-update) | async-done | bytes 524304 | tf_op jit(solution)/shard_map/reduce_scatter | solution.py:48
  185.5 2.0 %multiply_convert_fusion = bf16[128,1024]{1,0:T(8,128)(2,1)} fusion(f32[128,1024]{1,0:T(8,128)} %reduce-scatter.2.cloned.1.call-done, f32[2048,1024]{1,0:T(8,128)} %fusion.4, s32[]{:T(128)S(6)} %select_n.3), kind=kLoop, calls=%fused_computation.11 | loop fusion | flops 262144 | bytes 1310724 | tf_op jit(solution)/shard_map/convert_element_type | solution.py:50
Async XLA Ops:
  7.2 70.9 %copy-start = (bf16[1024,1024]{1,0:T(8,128)(2,1)S(1)}, bf16[1024,1024]{1,0:T(8,128)(2,1)}, u32[]{:S(2)}) copy-start(bf16[1024,1024]{1,0:T(8,128)(2,1)} %param.7) | copy-start | bytes 6291460
  7.2 63.3 %all-gather.4.cloned.1.call-start = ((), (), s32[]{:S(2)}) async-start(), calls=%async_computation.2 | async-start | bytes 4456448 | tf_op jit(solution)/shard_map/all_gather | solution.py:32
  7.9 106.6 %all-gather.6.cloned.1.call-start = ((), (), s32[]{:S(2)}) async-start(), calls=%async_computation.4 | async-start | bytes 4456448 | tf_op jit(solution)/shard_map/all_gather | solution.py:31
  8.7 176.8 %reduce-scatter.2.cloned.1.call-start = ((), (), s32[]{:S(2)}) async-start(), calls=%async_computation.3 | async-start | bytes 8912896 | tf_op jit(solution)/shard_map/reduce_scatter | solution.py:48
  76.1 2.0 %copy-start.2 = (bf16[2048,1024]{1,0:T(8,128)(2,1)}, bf16[2048,1024]{1,0:T(8,128)(2,1)S(1)}, u32[]{:S(2)}) copy-start(bf16[2048,1024]{1,0:T(8,128)(2,1)S(1)} %fusion) | copy-start | bytes 12582916
  85.1 0.7 copy-start.4
  85.1 0.8 copy-start.5
  114.5 7.7 %copy-start.1 = (bf16[2048,1024]{1,0:T(8,128)(2,1)S(1)}, bf16[2048,1024]{1,0:T(8,128)(2,1)}, u32[]{:S(2)}) copy-start(bf16[2048,1024]{1,0:T(8,128)(2,1)} %all-gather.4.cloned.1.call-done) | copy-start | bytes 12582916
  126.6 44.7 %all-to-all-start = ((f32[16,8,1024]{2,1,0:T(8,128)}), f32[16,8,1024]{2,1,0:T(8,128)S(1)}, u32[]{:S(2)}, u32[]{:S(2)}) async-start(f32[16,8,1024]{2,1,0:T(8,128)} %broadcast_in_dim.2), calls=%async_computation.1 | async-start | bytes 1048576 | tf_op jit(solution)/shard_map/all_to_all | solution.py:11
  133.1 13.0 %copy-start.3 = (bf16[2048,1024]{1,0:T(8,128)(2,1)S(1)}, bf16[2048,1024]{1,0:T(8,128)(2,1)}, u32[]{:S(2)}) copy-start(bf16[2048,1024]{1,0:T(8,128)(2,1)} %all-gather.6.cloned.1.call-done) | copy-start | bytes 12582916
Sparse Core Ops, SparseCore 0:
  10.4 60.0 all-gather.3
  72.3 42.1 all-gather.5
  117.1 68.3 reduce-scatter.1
where the time goes:
time: 196 us; the launch traced here: 194 us
  waiting for transfers between devices  99.8 us (51%)
  matrix products  48.2 us (25%)
  blocking collectives  18.7 us (10%)
  between operations  13.8 us (7%)
  starting transfers between devices  6.65 us (3%)
  local copies, waits for them, and re-layouts  3.59 us (2%)
  other arithmetic  3.25 us (2%)
    all_gather x1, waiting for transfers between devices, local(): full_cot = lax.all_gather(cotangent, 'row', axis=0, tiled=True)  61.8 us
    all_gather x1, waiting for transfers between devices, local(): full_inputs = lax.all_gather(inputs, 'col', axis=0, tiled=True)  23 us
    all_gather x1, blocking collectives, gathered_total(): return lax.all_gather(value, axis).sum(0)  18.7 us
    reduce_scatter x1, waiting for transfers between devices, local(): lax.psum_scatter(back_part, 'col', scatter_dimension=0, tiled=True)  13.6 us
    dot_general x1, matrix products, local(): lax.dot_general(scaled_in, scaled_cot, (((0,), (0,)), ((), ())), preferre...  13 us
    dot_general x2, matrix products, member_sums(): return jnp.dot(one_hot.T, values, precision=highest)  9.21 us
    dot_general x1, matrix products, local(): pre_part = jnp.dot(scaled_in, weight, preferred_element_type=jnp.float32)  7.7 us
    dot_general x1, matrix products, local(): lax.dot_general(scaled_cot, weight, (((1,), (1,)), ((), ())), preferred_e...  7.06 us
  transfers between devices with their start and end apart: 4, of which 3 were waited for; matrix products, arithmetic and copies ran while one was open for 26% of the time, Pallas kernels for 0%

commit v1 on v0

v1 whole, which is shorter than its diff:
```python
import jax
import jax.numpy as jnp
from jax import lax
from jax.experimental import pallas as pl
from jax.experimental.pallas import tpu as pltpu
from jax.sharding import PartitionSpec as P

MESH = pl.DeviceIdType.MESH
BF16 = jnp.bfloat16
F32 = jnp.float32
XN, YN, ZN = 4, 4, 8
ROWS = 128
HALF = 64
QUARTER = 32
BLOCKS = 16
NT = (((1,), (1,)), ((), ()))
TN = (((0,), (0,)), ((), ()))


def kernel(
    x_hbm, w_hbm, cot_hbm, sin_hbm, sout_hbm, mem_hbm,
    ig_hbm, wg_hbm, inf_hbm, outf_hbm,
    X, C, Xs, Cs, W, WT, pall, prx, sb, rb, wgs, r_own, ig_v,
    sin_v, sout_v, mem_v, sc_in, sc_out,
    acc_in, acc_in_rx, fz, fin, acc_out, fx, fy, fout,
    load_sem, store_sem,
    a_s, a_r, pa_s, pa_r, b_s, b_r, d_s, d_r, c_s, c_r,
    fp_s, fp_r, fz_s, fz_r, fh_s, fh_r, fx_s, fx_r, fy_s, fy_r,
):
    row, col = lax.axis_index("row"), lax.axis_index("col")
    x, y = lax.div(row, YN), lax.rem(row, YN)
    z, c = lax.div(col, 2), lax.rem(col, 2)
    depth, width = W.shape

    def zi(k):
        return lax.rem(z + (k % ZN), ZN)

    def at(dx, dy):
        return YN * lax.rem(x + dx, XN) + lax.rem(y + dy, YN)

    def z_dev(k):
        return (row, 2 * zi(k) + c)

    partner = (row, 2 * z + 1 - c)

    def x_dev(k):
        return (at(k % XN, 0), col)

    def y_dev(k):
        return (at(0, k % YN), col)

    def rows(block, offset=0, size=ROWS):
        return pl.ds(pl.multiple_of(block * ROWS + offset, QUARTER), size)

    def remote(src, dst, send, recv, dev):
        return pltpu.make_async_remote_copy(
            src_ref=src, dst_ref=dst, send_sem=send, recv_sem=recv,
            device_id=dev, device_id_type=MESH,
        )

    def a_copy(d, u, recv=0):
        sign = 1 - 2 * d
        block = 2 * zi(-sign * (u // 2 + recv)) + c
        half = u % 2 if d == 0 else 1 - u % 2
        part = X.at[rows(block, HALF * half, HALF)]
        return remote(part, part, a_s.at[d, u], a_r.at[d, u], z_dev(sign))

    def pa_copy(k, recv=0):
        part = X.at[rows(2 * zi(k) + ((1 - c) if recv else c))]
        return remote(part, part, pa_s.at[k], pa_r.at[k], partner)

    def b_block(h, da, db):
        da, db = da % 4, db % 4
        return at(da, db) if h == 0 else at(db, da)

    def b_dev(h, axis, sign):
        along_x = (axis == 0) == (h == 0)
        return x_dev(sign) if along_x else y_dev(sign)

    OFF = (0, -1, 1, 2)

    def b_copy(h, kind, d, s=0, recv=0):
        sign = 1 - 2 * d
        if kind == "first":
            index, block, axis, off, size = d, b_block(h, -sign * recv, 0), 0, 0, HALF
        elif kind == "first_q":
            index, block, axis = 2 + d, b_block(h, -sign * (1 + recv), 0), 0
            off, size = QUARTER * d, QUARTER
        elif kind == "second":
            index, block, axis = 4 + 2 * s + d, b_block(h, OFF[s], -sign * recv), 1
            off, size = 0, HALF
        else:
            index, block, axis = 12 + 2 * s + d, b_block(h, OFF[s], -sign * (1 + recv)), 1
            off, size = QUARTER * d, QUARTER
        part = C.at[rows(block, HALF * h + off, size)]
        return remote(part, part, b_s.at[h, index], b_r.at[h, index], b_dev(h, axis, sign))

    def d_copy(pair, recv=0):
        src = pall.at[rows(2 * pair + ((c) if recv else (1 - c)))]
        return remote(src, prx.at[rows(pair)], d_s.at[pair], d_r.at[pair], partner)

    def c_copy(d, u):
        return remote(sb.at[d, u], rb.at[d, u], c_s.at[d, u], c_r.at[d, u], z_dev(1 - 2 * d))

    both = (0, 1)

    def one_hot_t(block, copies):
        members = mem_v[pl.ds(block, 1), :]
        ids = lax.broadcasted_iota(jnp.int32, (copies, ROWS), 0)
        hit = (lax.rem(ids, 8) == members) & (ids < 24)
        return jnp.where(hit, 1.0, 0.0).astype(BF16)

    def member_rows(block, sc):
        return lax.dot_general(one_hot_t(block, 32), sc[...], TN, preferred_element_type=F32)

    def split(v, out):
        s = v[...]
        hi = s.astype(BF16).astype(F32)
        mid = (s - hi).astype(BF16).astype(F32)
        low = s - hi - mid
        out[...] = jnp.concatenate([hi, mid, low, jnp.zeros_like(s)], axis=0).astype(BF16)

    def scale_in_block(block):
        Xs[rows(block)] = (X[rows(block)].astype(F32) * member_rows(block, sc_in)).astype(BF16)

    def back_block(block):
        Cs[rows(block)] = (C[rows(block)].astype(F32) * member_rows(block, sc_out)).astype(BF16)
        lhs = Cs[rows(block)]
        for n in range(depth // 256):
            cols = pl.ds(256 * n, 256)
            pall[rows(block), cols] = jnp.dot(
                lhs, WT[:, cols], preferred_element_type=F32
            ).astype(BF16)

        @pl.when(lax.rem(block, 2) != c)
        def _():
            pair = lax.div(block, 2)
            d_copy(pair).start()

    def back_group(count, offsets):
        def body(i, carry):
            dx, dy = offsets(i)
            back_block(at(dx, dy))
            return carry
        lax.fori_loop(0, count, body, 0)

    loads = [
        pltpu.make_async_copy(x_hbm, X.at[rows(col)], load_sem.at[0]),
        pltpu.make_async_copy(cot_hbm, C.at[rows(row)], load_sem.at[1]),
        pltpu.make_async_copy(w_hbm, W, load_sem.at[2]),
        pltpu.make_async_copy(sin_hbm, sin_v, load_sem.at[3]),
        pltpu.make_async_copy(sout_hbm, sout_v, load_sem.at[4]),
        pltpu.make_async_copy(mem_hbm, mem_v, load_sem.at[5]),
    ]
    for load in loads:
        load.start()
    barrier = pltpu.get_barrier_semaphore()
    for dev in (z_dev(1), z_dev(-1), x_dev(1), x_dev(-1), y_dev(1), y_dev(-1), partner):
        pl.semaphore_signal(barrier, inc=1, device_id=dev, device_id_type=MESH)
    pl.semaphore_wait(barrier, 7)

    loads[1].wait()
    for h in both:
        for d in both:
            b_copy(h, "first", d).start()
    loads[0].wait()
    for u in (0, 1):
        for d in both:
            a_copy(d, u).start()
    for h in both:
        for d in both:
            b_copy(h, "second", d, 0).start()
    pa_copy(0).start()
    for load in loads[2:]:
        load.wait()
    split(sin_v, sc_in)
    split(sout_v, sc_out)

    def transpose_step(i, carry):
        src = pl.ds(pl.multiple_of(i * 128, 128), 128)
        for k in range(width // 256):
            WT[pl.ds(256 * k, 256), src] = W[src, pl.ds(256 * k, 256)].T
        return carry
    lax.fori_loop(0, depth // 128, transpose_step, 0)

    def a_tick(u, forward):
        for d in both:
            a_copy(d, u, 1).wait_recv()
            if forward:
                a_copy(d, u + 2).start()

    def pa_send(*ks):
        for k in ks:
            pa_copy(k).start()

    a_tick(0, True)
    for h in both:
        for d in both:
            b_copy(h, "first", d, recv=1).wait_recv()
            b_copy(h, "first_q", d).start()
    for h in both:
        for s in (1, 2):
            for d in both:
                b_copy(h, "second", d, s).start()
    back_group(1, lambda i: (0, 0))
    scale_in_block(col)

    a_tick(1, True)
    pa_send(1, 7)
    for h in both:
        for d in both:
            b_copy(h, "second", d, 0, recv=1).wait_recv()
            b_copy(h, "second_q", d, 0).start()
    back_group(2, lambda i: (1 + 2 * i, 0))

    for h in both:
        for d in both:
            b_copy(h, "first_q", d, recv=1).wait_recv()
        for d in both:
            b_copy(h, "second", d, 3).start()
    back_group(2, lambda i: (0, 1 + 2 * i))

    a_tick(2, True)
    for h in both:
        for d in both:
            b_copy(h, "second_q", d, 0, recv=1).wait_recv()
    back_group(2, lambda i: (2 - 2 * i, 2 * i))

    a_tick(3, True)
    pa_send(2, 6)

    for h in both:
        for s in (1, 2):
            for d in both:
                b_copy(h, "second", d, s, recv=1).wait_recv()
                b_copy(h, "second_q", d, s).start()
    back_group(2, lambda i: (1, 1 + 2 * i))

    a_tick(4, True)
    back_group(2, lambda i: (3, 1 + 2 * i))

    a_tick(5, False)
    pa_send(3, 5)
    for h in both:
        for d in both:
            b_copy(h, "second", d, 3, recv=1).wait_recv()
            b_copy(h, "second_q", d, 3).start()

    def scale_landed(pair):
        pa_copy(pair, 1).wait_recv()

    a_tick(6, False)
    pa_send(4)
    for h in both:
        for s in (1, 2):
            for d in both:
                b_copy(h, "second_q", d, s, recv=1).wait_recv()
    back_group(4, lambda i: (
        2 * (1 - lax.div(i, 2)) + lax.div(i, 2) * (1 + 2 * lax.rem(i, 2)),
        2 * lax.div(i, 2) + (1 - lax.div(i, 2)) * (1 + 2 * lax.rem(i, 2)),
    ))
    for h in both:
        for d in both:
            b_copy(h, "second_q", d, 3, recv=1).wait_recv()
    back_group(1, lambda i: (2, 2))

    def chip_sum(k, half=0, size=ROWS):
        pair = zi(k)
        own = pall[rows(2 * pair + c, HALF * half, size)].astype(F32)
        return own + prx[rows(pair, HALF * half, size)].astype(F32)

    def c_tick(u):
        k = 4 - (u + 1) // 2
        for d in both:
            half = u % 2 if d == 0 else 1 - u % 2
            if u >= 2:
                c_copy(d, u - 2).wait_recv()
            total = chip_sum(k if d == 0 else -k, half, HALF)
            if u >= 2:
                total += rb[d, u - 2].astype(F32)
            sb[d, u] = total.astype(BF16)
            c_copy(d, u).start()

    def d_wait(*ks):
        for k in ks:
            d_copy(zi(k), 1).wait_recv()

    def pre_piece(i, carry):
        two = pl.ds(pl.multiple_of(i * 256, 256), 256)
        lhs = Xs[two]
        hot = jnp.concatenate([one_hot_t(2 * i, 16), one_hot_t(2 * i + 1, 16)], axis=1)
        for n in range(width // 256):
            cols = pl.ds(256 * n, 256)
            pre = jnp.dot(lhs, W[:, cols], preferred_element_type=F32)
            term = (C[two, cols].astype(F32) * pre).astype(BF16)
            acc_out[:, cols] += jnp.dot(hot, term, preferred_element_type=F32)
        return carry

    def in_piece(k, carry):
        pair = lax.rem(z + k, ZN)
        block = 2 * pair + c
        hot = one_hot_t(block, 16)
        for n in range(depth // 256):
            cols = pl.ds(256 * n, 256)
            total = pall[rows(block), cols].astype(F32) + prx[rows(pair), cols].astype(F32)
            term = (X[rows(block), cols].astype(F32) * total).astype(BF16)
            acc_in[:, cols] += jnp.dot(hot, term, preferred_element_type=F32)
        return carry

    def wg_piece(i):
        cols = pl.ds(256 * i, 256)
        for n in range(width // 256):
            wgs[cols, pl.ds(256 * n, 256)] = lax.dot_general(
                Xs[:, cols], Cs[:, pl.ds(256 * n, 256)], TN, preferred_element_type=F32
            )
        pltpu.make_async_copy(wgs.at[cols], wg_hbm.at[cols], store_sem.at[i]).start()

    acc_in[...] = jnp.zeros_like(acc_in)
    acc_out[...] = jnp.zeros_like(acc_out)
    d_wait(4, 3, 5)
    c_tick(0)
    c_tick(1)
    for k in range(ZN):
        pa_copy(k, 1).wait_recv()

    def scale_step(i, carry):
        scale_in_block(i)
        return carry
    d_wait(2, 6, 1, 7, 0)
    lax.fori_loop(0, BLOCKS, scale_step, 0)
    c_tick(2)
    lax.fori_loop(0, ZN, in_piece, 0)
    in_swap = remote(acc_in, acc_in_rx, fp_s.at[0], fp_r.at[0], partner)
    in_swap.start()
    lax.fori_loop(0, 2, pre_piece, 0)
    c_tick(3)
    in_swap.wait_recv()

    my_half = pl.ds(pl.multiple_of(c * (depth // 2), depth // 2), depth // 2)
    other_half = pl.ds(pl.multiple_of((1 - c) * (depth // 2), depth // 2), depth // 2)
    fz[z] = acc_in[:8, my_half] + acc_in_rx[:8, my_half]

    def fz_copy(d, u, recv=0):
        sign = 1 - 2 * d
        slot = fz.at[zi(-sign * (u + recv))]
        return remote(slot, slot, fz_s.at[d, u], fz_r.at[d, u], z_dev(sign))

    fz_copy(0, 0).start()
    fz_copy(1, 0).start()
    lax.fori_loop(2, 5, pre_piece, 0)
    c_tick(4)
    for d in both:
        fz_copy(d, 0, 1).wait_recv()
        fz_copy(d, 1).start()
    lax.fori_loop(5, 8, pre_piece, 0)

    def fx_copy(i, recv=0):
        sign = -1 if i == 1 else 1
        slot = fx.at[lax.rem(x + ((-sign * recv - (i == 2)) % XN), XN)]
        return remote(slot, slot, fx_s.at[i], fx_r.at[i], x_dev(sign))

    def fy_copy(i, recv=0):
        sign = -1 if i == 1 else 1
        slot = fy.at[lax.rem(y + ((-sign * recv - (i == 2)) % YN), YN)]
        return remote(slot, slot, fy_s.at[i], fy_r.at[i], y_dev(sign))

    fx[x] = acc_out[:8, :]
    fx_copy(0).start()
    fx_copy(1).start()
    c_tick(5)
    for d in both:
        fz_copy(d, 1, 1).wait_recv()
        fz_copy(d, 2).start()
    wg_piece(0)
    fx_copy(0, 1).wait_recv()
    fx_copy(2).start()
    wg_piece(1)
    c_tick(6)
    for d in both:
        fz_copy(d, 2, 1).wait_recv()
    fz_copy(0, 3).start()
    fx_copy(1, 1).wait_recv()
    fx_copy(2, 1).wait_recv()
    fy[y] = ((fx[0] + fx[1]) + fx[2]) + fx[3]
    fy_copy(0).start()
    fy_copy(1).start()
    wg_piece(2)
    fy_copy(0, 1).wait_recv()
    fy_copy(2).start()
    wg_piece(3)
    r_own[...] = member_rows(col, sc_in)

    fz_copy(0, 3, 1).wait_recv()
    total_in = fz[0]
    for k in range(1, ZN):
        total_in += fz[k]
    fin[:, my_half] = total_in
    half_swap = remote(fin.at[:, my_half], fin.at[:, my_half], fh_s.at[0], fh_r.at[0], partner)
    half_swap.start()
    half_back = remote(fin.at[:, other_half], fin.at[:, other_half], fh_s.at[0], fh_r.at[0], partner)

    fy_copy(1, 1).wait_recv()
    fy_copy(2, 1).wait_recv()
    fout[...] = ((fy[0] + fy[1]) + fy[2]) + fy[3]
    store_out = pltpu.make_async_copy(fout, outf_hbm, store_sem.at[4])
    store_out.start()
    half_back.wait_recv()
    store_in = pltpu.make_async_copy(fin, inf_hbm, store_sem.at[5])
    store_in.start()

    for d in both:
        c_copy(d, 5).wait_recv()
    for d in both:
        c_copy(d, 6).wait_recv()
    for half in both:
        part = pl.ds(HALF * half, HALF)
        total = chip_sum(0, half, HALF)
        total += rb[0, 6 - half].astype(F32) + rb[1, 5 + half].astype(F32)
        ig_v[part] = (total * r_own[part]).astype(BF16)
    store_ig = pltpu.make_async_copy(ig_v, ig_hbm, store_sem.at[6])
    store_ig.start()

    for d in both:
        for u in range(7):
            a_copy(d, u).wait_send()
            c_copy(d, u).wait_send()
    for k in range(ZN):
        pa_copy(k).wait_send()
        d_copy(k).wait_send()
    for h in both:
        for d in both:
            b_copy(h, "first", d).wait_send()
            b_copy(h, "first_q", d).wait_send()
            for s in range(4):
                b_copy(h, "second", d, s).wait_send()
                b_copy(h, "second_q", d, s).wait_send()
    in_swap.wait_send()
    half_swap.wait_send()
    for u in range(3):
        fx_copy(u).wait_send()
        fy_copy(u).wait_send()
        for d in both:
            fz_copy(d, u).wait_send()
    fz_copy(0, 3).wait_send()
    for i in range(4):
        cols = pl.ds(256 * i, 256)
        pltpu.make_async_copy(wgs.at[cols], wg_hbm.at[cols], store_sem.at[i]).wait()
    store_out.wait()
    store_in.wait()
    store_ig.wait()


def local(inputs, weight, cotangent, scale_in, scale_out, member):
    depth, width = weight.shape
    batch = BLOCKS * ROWS
    anywhere = pl.BlockSpec(memory_space=pl.ANY)
    dma = pltpu.SemaphoreType.DMA
    return pl.pallas_call(
        kernel,
        out_shape=(
            jax.ShapeDtypeStruct((ROWS, depth), BF16),
            jax.ShapeDtypeStruct((depth, width), F32),
            jax.ShapeDtypeStruct((8, depth), F32),
            jax.ShapeDtypeStruct((8, width), F32),
        ),
        in_specs=[anywhere] * 6,
        out_specs=(anywhere,) * 4,
        scratch_shapes=[
            pltpu.VMEM((batch, depth), BF16),
            pltpu.VMEM((batch, width), BF16),
            pltpu.VMEM((batch, depth), BF16),
            pltpu.VMEM((batch, width), BF16),
            pltpu.VMEM((depth, width), BF16),
            pltpu.VMEM((width, depth), BF16),
            pltpu.VMEM((batch, depth), BF16),
            pltpu.VMEM((batch // 2, depth), BF16),
            pltpu.VMEM((2, 7, HALF, depth), BF16),
            pltpu.VMEM((2, 7, HALF, depth), BF16),
            pltpu.VMEM((depth, width), F32),
            pltpu.VMEM((ROWS, depth), F32),
            pltpu.VMEM((ROWS, depth), BF16),
            pltpu.VMEM((8, depth), F32),
            pltpu.VMEM((8, width), F32),
            pltpu.VMEM((BLOCKS, ROWS), jnp.int32),
            pltpu.VMEM((32, depth), BF16),
            pltpu.VMEM((32, width), BF16),
            pltpu.VMEM((16, depth), F32),
            pltpu.VMEM((16, depth), F32),
            pltpu.VMEM((ZN, 8, depth // 2), F32),
            pltpu.VMEM((8, depth), F32),
            pltpu.VMEM((16, width), F32),
            pltpu.VMEM((XN, 8, width), F32),
            pltpu.VMEM((YN, 8, width), F32),
            pltpu.VMEM((8, width), F32),
            dma((6,)), dma((7,)),
            dma((2, 7)), dma((2, 7)), dma((8,)), dma((8,)),
            dma((2, 20)), dma((2, 20)), dma((8,)), dma((8,)),
            dma((2, 7)), dma((2, 7)),
            dma((1,)), dma((1,)), dma((2, 4)), dma((2, 4)),
            dma((1,)), dma((1,)), dma((3,)), dma((3,)), dma((3,)), dma((3,)),
        ],
        compiler_params=pltpu.CompilerParams(
            collective_id=0, has_side_effects=True, vmem_limit_bytes=60 * 1024 * 1024
        ),
    )(inputs, weight, cotangent, scale_in, scale_out, member.reshape(BLOCKS, ROWS))


def solution(mesh):
    placed = (
        P("col", "row"),
        P("row", "col"),
        P("row", "col"),
        P(None, "row"),
        P(None, "col"),
        P(),
    )
    return jax.shard_map(
        local,
        mesh=mesh,
        in_specs=placed,
        out_specs=(P("col", "row"), P("row", "col"), P(None, "row"), P(None, "col")),
        check_vma=False,
    )
```

time: 196 us -> 83.4 us (0.43)
  waiting for transfers between devices: 99.8 us -> 0 us
  Pallas kernels: 0 us -> 74.9 us
  matrix products: 48.2 us -> 0 us
  blocking collectives: 18.7 us -> 0 us
  between operations: 13.8 us -> 0.64 us
  starting transfers between devices: 6.65 us -> 0 us
  local copies, waits for them, and re-layouts: 3.59 us -> 7.7 us
  other arithmetic: 3.25 us -> 0 us
    all_gather x2 -> x0, waiting for transfers between devices: 84.8 us -> none  [the longest x1 61.8 us: local(): full_cot = lax.all_gather(cotangent, 'row', axis=0, tiled=True)]
    pallas_call x0 -> x1, Pallas kernels: none -> 74.9 us  [local(): pl.pallas_call(kernel, out_shape=(jax.ShapeDtypeStruct((ROWS, depth), BF1...]
    dot_general x7 -> x0, matrix products: 48.2 us -> none  [the longest x1 13 us: local(): lax.dot_general(scaled_in, scaled_cot, (((0,), (0,)), ((), ())), preferre...]
    all_gather x1 -> x0, blocking collectives: 18.7 us -> none  [gathered_total(): return lax.all_gather(value, axis).sum(0)]
    reduce_scatter x1 -> x0, waiting for transfers between devices: 13.6 us -> none  [local(): lax.psum_scatter(back_part, 'col', scatter_dimension=0, tiled=True)]
    all_to_all x1 -> x0, starting transfers between devices: 6.54 us -> none  [from_everyone(): return lax.all_to_all(copies, axis, split_axis=0, concat_axis=0, tiled=True)]
    unnamed x12 -> x8, local copies, waits for them, and re-layouts: 2.71 us -> 7.7 us
    convert_element_type x1 -> x0, other arithmetic: 1.96 us -> none  [local(): input_grad = (back_block * r_block).astype(jnp.bfloat16)]
  transfers between devices with their start and end apart: 4 -> 0, of which waited for: 3 -> 0; matrix products, arithmetic and copies ran while one was open for 26% -> 0% of each run, Pallas kernels for 0% -> 0%
where the time goes in v1:
time: 83.4 us; the launch traced here: 83.3 us
  Pallas kernels  74.9 us (90%)
  local copies, waits for them, and re-layouts  7.7 us (9%)
    pallas_call x1, Pallas kernels, local(): pl.pallas_call(kernel, out_shape=(jax.ShapeDtypeStruct((ROWS, depth), BF1...  74.9 us
    unnamed x8, local copies, waits for them, and re-layouts  7.7 us

profile of v1, /device:TPU:1, one launch (start us, length us, event | category | flops | bytes accessed | tf_op | source)
XLA Modules:
  0.0 83.3 jit_solution(16154166691918896540)
XLA Ops:
  0.6 74.9 %shard_map.93 = (bf16[128,1024]{1,0:T(8,128)(2,1)}, f32[1024,1024]{1,0:T(8,128)}, f32[8,1024]{1,0:T(8,128)}, f32[8,1024]{1,0:T(8,128)}) custom-call(bf16[128,1024]{1,0:T(8,128)(2,1)} %x_hbm.1, bf16[1024,1024]{1,0:T(8,128)(2,1)} %w_hbm.1, bf16[128,1024]{1,0:T(8,128)(2,1)} %cot_hbm.1, f32[8,1024]{1,0:T(8,128)} %sin_hbm.1, f32[8,1024]{1,0:T(8,128)} %sout_hbm.1, ...), custom_call_target="tpu_custom_call" | custom-call | tf_op jit(solution)/shard_map/pallas_call | solution.py:458
  75.6 1.7 %copy.14 = bf16[128,1024]{1,0:T(8,128)(2,1)} copy(bf16[128,1024]{1,0:T(8,128)(2,1)} %get-tuple-element.8) | data formatting | bytes 524288
  77.2 0.0 copy-start.1
  77.2 0.0 copy-start
  77.2 4.8 %copy.15 = f32[1024,1024]{1,0:T(8,128)} copy(f32[1024,1024]{1,0:T(8,128)} %get-tuple-element.9) | data formatting | bytes 8388608
  82.0 0.0 copy-done.1
  82.0 0.6 copy.16
  82.7 0.0 copy-done
  82.7 0.6 copy.17
Async XLA Ops:
  77.2 4.8 %copy-start.1 = (f32[8,1024]{1,0:T(8,128)S(1)}, f32[8,1024]{1,0:T(8,128)}, u32[]{:S(2)}) copy-start(f32[8,1024]{1,0:T(8,128)} %get-tuple-element.10) | copy-start | bytes 98308
  77.2 5.4 %copy-start = (f32[8,1024]{1,0:T(8,128)S(1)}, f32[8,1024]{1,0:T(8,128)}, u32[]{:S(2)}) copy-start(f32[8,1024]{1,0:T(8,128)} %get-tuple-element.11) | copy-start | bytes 98308

commit v2 on v1

v2 whole, which is shorter than its diff:
```python
import jax
import jax.numpy as jnp
from jax import lax
from jax.experimental import pallas as pl
from jax.experimental.pallas import tpu as pltpu
from jax.sharding import PartitionSpec as P

MESH = pl.DeviceIdType.MESH
BF16 = jnp.bfloat16
F32 = jnp.float32
XN, YN, ZN = 4, 4, 8
ROWS = 128
HALF = 64
QUARTER = 32
BLOCKS = 16
TN = (((0,), (0,)), ((), ()))


def kernel(
    x_hbm, w_hbm, cot_hbm, sin_hbm, sout_hbm, mem_hbm,
    ig_v, wgs, fin, fout,
    X, C, Xs, Cs, W, WT, pall, prx, sb, rb, r_own,
    sin_v, sout_v, mem_v, sc_in, sc_out,
    hot, hot_c, terms, in_terms, acc_in, acc_in_rx, fz, fx, fy,
    load_sem,
    a_s, a_r, pa_s, pa_r, b_s, b_r, d_s, d_r, c_s, c_r,
    fp_s, fp_r, fz_s, fz_r, fh_s, fh_r, fx_s, fx_r, fy_s, fy_r,
):
    row, col = lax.axis_index("row"), lax.axis_index("col")
    x, y = lax.div(row, YN), lax.rem(row, YN)
    z, c = lax.div(col, 2), lax.rem(col, 2)
    depth, width = W.shape

    def zi(k):
        return lax.rem(z + (k % ZN), ZN)

    def at(dx, dy):
        return YN * lax.rem(x + dx, XN) + lax.rem(y + dy, YN)

    def z_dev(k):
        return (row, 2 * zi(k) + c)

    partner = (row, 2 * z + 1 - c)

    def x_dev(k):
        return (at(k % XN, 0), col)

    def y_dev(k):
        return (at(0, k % YN), col)

    def rows(block, offset=0, size=ROWS):
        return pl.ds(pl.multiple_of(block * ROWS + offset, QUARTER), size)

    def lanes(block):
        return pl.ds(pl.multiple_of(block * ROWS, ROWS), ROWS)

    def remote(src, dst, send, recv, dev):
        return pltpu.make_async_remote_copy(
            src_ref=src, dst_ref=dst, send_sem=send, recv_sem=recv,
            device_id=dev, device_id_type=MESH,
        )

    def a_copy(d, u, recv=0):
        sign = 1 - 2 * d
        block = 2 * zi(-sign * (u // 2 + recv)) + c
        half = u % 2 if d == 0 else 1 - u % 2
        part = X.at[rows(block, HALF * half, HALF)]
        return remote(part, part, a_s.at[d, u], a_r.at[d, u], z_dev(sign))

    def pa_copy(k, recv=0):
        part = X.at[rows(2 * zi(k) + ((1 - c) if recv else c))]
        return remote(part, part, pa_s.at[k], pa_r.at[k], partner)

    def b_block(h, da, db):
        da, db = da % 4, db % 4
        return at(da, db) if h == 0 else at(db, da)

    def b_dev(h, axis, sign):
        along_x = (axis == 0) == (h == 0)
        return x_dev(sign) if along_x else y_dev(sign)

    OFF = (0, -1, 1, 2)

    def b_copy(h, kind, d, s=0, recv=0):
        sign = 1 - 2 * d
        if kind == "first":
            index, block, axis, off, size = d, b_block(h, -sign * recv, 0), 0, 0, HALF
        elif kind == "first_q":
            index, block, axis = 2 + d, b_block(h, -sign * (1 + recv), 0), 0
            off, size = QUARTER * d, QUARTER
        elif kind == "second":
            index, block, axis = 4 + 2 * s + d, b_block(h, OFF[s], -sign * recv), 1
            off, size = 0, HALF
        else:
            index, block, axis = 12 + 2 * s + d, b_block(h, OFF[s], -sign * (1 + recv)), 1
            off, size = QUARTER * d, QUARTER
        part = C.at[rows(block, HALF * h + off, size)]
        return remote(part, part, b_s.at[h, index], b_r.at[h, index], b_dev(h, axis, sign))

    def d_copy(pair, recv=0):
        src = pall.at[rows(2 * pair + ((c) if recv else (1 - c)))]
        return remote(src, prx.at[rows(pair)], d_s.at[pair], d_r.at[pair], partner)

    def c_copy(d, u):
        return remote(sb.at[d, u], rb.at[d, u], c_s.at[d, u], c_r.at[d, u], z_dev(1 - 2 * d))

    both = (0, 1)

    def make_hot(i, carry):
        members = mem_v[pl.ds(i, 1), :]
        ids = lax.broadcasted_iota(jnp.int32, (32, ROWS), 0)
        hit = (lax.rem(ids, 8) == members) & (ids < 24)
        hot[:, lanes(i)] = jnp.where(hit, 1.0, 0.0).astype(BF16)
        return carry

    def member_rows(blocks, sc):
        ones = [hot[:, lanes(block)] for block in blocks]
        ones = ones[0] if len(ones) == 1 else jnp.concatenate(ones, axis=1)
        return lax.dot_general(ones, sc[...], TN, preferred_element_type=F32)

    def split(v, out):
        s = v[...]
        hi = s.astype(BF16).astype(F32)
        mid = (s - hi).astype(BF16).astype(F32)
        low = s - hi - mid
        out[...] = jnp.concatenate([hi, mid, low, jnp.zeros_like(s)], axis=0).astype(BF16)

    def scale(blocks, src, sc, dst):
        factor = member_rows(blocks, sc)
        for i, block in enumerate(blocks):
            part = factor[ROWS * i : ROWS * (i + 1)]
            dst[rows(block)] = (src[rows(block)].astype(F32) * part).astype(BF16)

    def back_blocks(*places):
        blocks = [at(dx, dy) for dx, dy in places]
        scale(blocks, C, sc_out, Cs)
        lhs = [Cs[rows(block)] for block in blocks]
        lhs = lhs[0] if len(lhs) == 1 else jnp.concatenate(lhs, axis=0)
        for n in range(depth // 256):
            cols = pl.ds(256 * n, 256)
            product = jnp.dot(lhs, WT[:, cols], preferred_element_type=F32).astype(BF16)
            for i, block in enumerate(blocks):
                pall[rows(block), cols] = product[ROWS * i : ROWS * (i + 1)]
        for block in blocks:
            @pl.when(lax.rem(block, 2) != c)
            def _():
                d_copy(lax.div(block, 2)).start()

    def pre_pair(k, landed):
        pair = zi(k)
        scale([2 * pair, 2 * pair + 1], X, sc_in, Xs)
        two = rows(2 * pair, 0, 2 * ROWS)
        lhs = Xs[two]
        for n in range(width // 256):
            cols = pl.ds(256 * n, 256)
            pre = jnp.dot(lhs, W[:, cols], preferred_element_type=F32)
            if landed:
                pre = C[two, cols].astype(F32) * pre
            terms[two, cols] = pre.astype(BF16)

    loads = [
        pltpu.make_async_copy(x_hbm, X.at[rows(col)], load_sem.at[0]),
        pltpu.make_async_copy(cot_hbm, C.at[rows(row)], load_sem.at[1]),
        pltpu.make_async_copy(w_hbm, W, load_sem.at[2]),
        pltpu.make_async_copy(sin_hbm, sin_v, load_sem.at[3]),
        pltpu.make_async_copy(sout_hbm, sout_v, load_sem.at[4]),
        pltpu.make_async_copy(mem_hbm, mem_v, load_sem.at[5]),
    ]
    for load in loads:
        load.start()
    barrier = pltpu.get_barrier_semaphore()
    for dev in (z_dev(1), z_dev(-1), x_dev(1), x_dev(-1), y_dev(1), y_dev(-1), partner):
        pl.semaphore_signal(barrier, inc=1, device_id=dev, device_id_type=MESH)
    pl.semaphore_wait(barrier, 7)

    loads[1].wait()
    for h in both:
        for d in both:
            b_copy(h, "first", d).start()
    loads[0].wait()
    for u in (0, 1):
        for d in both:
            a_copy(d, u).start()
    for h in both:
        for d in both:
            b_copy(h, "second", d, 0).start()
    pa_copy(0).start()
    for load in loads[2:]:
        load.wait()
    split(sin_v, sc_in)
    split(sout_v, sc_out)
    lax.fori_loop(0, BLOCKS, make_hot, 0)

    def transpose_step(i, carry):
        src = pl.ds(pl.multiple_of(i * 128, 128), 128)
        for k in range(width // 256):
            WT[pl.ds(256 * k, 256), src] = W[src, pl.ds(256 * k, 256)].T
        return carry
    lax.fori_loop(0, depth // 128, transpose_step, 0)
    back_blocks((0, 0))

    def a_tick(u, forward=True):
        for d in both:
            a_copy(d, u, 1).wait_recv()
            if forward:
                a_copy(d, u + 2).start()

    def pa_send(*ks):
        for k in ks:
            pa_copy(k).start()

    def pa_wait(*ks):
        for k in ks:
            pa_copy(k, 1).wait_recv()

    def b_wait(kind, s=0):
        for h in both:
            for d in both:
                b_copy(h, kind, d, s, recv=1).wait_recv()

    a_tick(0)
    for h in both:
        for d in both:
            b_copy(h, "first", d, recv=1).wait_recv()
            b_copy(h, "first_q", d).start()
    for h in both:
        for s in (1, 2):
            for d in both:
                b_copy(h, "second", d, s).start()
    a_tick(1)
    pa_send(1, 7)
    for h in both:
        for d in both:
            b_copy(h, "second", d, 0, recv=1).wait_recv()
            b_copy(h, "second_q", d, 0).start()
    back_blocks((1, 0), (3, 0))

    for h in both:
        for d in both:
            b_copy(h, "first_q", d, recv=1).wait_recv()
        for d in both:
            b_copy(h, "second", d, 3).start()
    back_blocks((0, 1), (0, 3))

    a_tick(2)
    pa_wait(0)
    pre_pair(0, False)
    pa_wait(1)
    pre_pair(1, False)
    a_tick(3)
    pa_send(2, 6)
    for h in both:
        for s in (1, 2):
            for d in both:
                b_copy(h, "second", d, s, recv=1).wait_recv()
                b_copy(h, "second_q", d, s).start()
    back_blocks((1, 1), (1, 3))
    a_tick(4)
    b_wait("second_q", 0)
    back_blocks((2, 0), (0, 2))
    back_blocks((3, 1), (3, 3))

    a_tick(5, False)
    pa_send(3, 5)
    for h in both:
        for d in both:
            b_copy(h, "second", d, 3, recv=1).wait_recv()
            b_copy(h, "second_q", d, 3).start()
    pa_wait(7)
    pre_pair(-1, False)
    pa_wait(2)
    pre_pair(2, False)

    a_tick(6, False)
    pa_send(4)
    b_wait("second_q", 1)
    b_wait("second_q", 2)
    back_blocks((2, 1), (2, 3))
    back_blocks((1, 2), (3, 2))
    b_wait("second_q", 3)
    back_blocks((2, 2))

    def chip_sum(k, half=0, size=ROWS):
        pair = zi(k)
        own = pall[rows(2 * pair + c, HALF * half, size)].astype(F32)
        return own + prx[rows(pair, HALF * half, size)].astype(F32)

    def c_tick(u, relay=None):
        k = 4 - (u + 1) // 2
        for d in both:
            half = u % 2 if d == 0 else 1 - u % 2
            if u >= 2:
                c_copy(d, u - 2).wait_recv()
            total = chip_sum(k if d == 0 else -k, half, HALF)
            if u >= 2:
                total += rb[d, u - 2].astype(F32)
            sb[d, u] = total.astype(BF16)
            if relay is not None:
                relay(d)
            c_copy(d, u).start()

    def d_wait(*ks):
        for k in ks:
            d_copy(zi(k), 1).wait_recv()

    def in_piece(pair, carry):
        block = 2 * pair + c
        total = pall[rows(block)].astype(F32) + prx[rows(pair)].astype(F32)
        in_terms[rows(pair)] = (X[rows(block)].astype(F32) * total).astype(BF16)
        hot_c[:, lanes(pair)] = hot[:16, lanes(block)]
        return carry

    def wg_piece(i):
        cols = pl.ds(256 * i, 256)
        for n in range(width // 256):
            wgs[cols, pl.ds(256 * n, 256)] = lax.dot_general(
                Xs[:, cols], Cs[:, pl.ds(256 * n, 256)], TN, preferred_element_type=F32
            )

    my_half = pl.ds(pl.multiple_of(c * (depth // 2), depth // 2), depth // 2)
    other_half = pl.ds(pl.multiple_of((1 - c) * (depth // 2), depth // 2), depth // 2)
    in_swap = remote(acc_in, acc_in_rx, fp_s.at[0], fp_r.at[0], partner)
    half_swap = remote(fin.at[:, my_half], fin.at[:, my_half], fh_s.at[0], fh_r.at[0], partner)
    half_back = remote(fin.at[:, other_half], fin.at[:, other_half], fh_s.at[0], fh_r.at[0], partner)

    def fz_copy(d, u, recv=0):
        sign = 1 - 2 * d
        slot = fz.at[zi(-sign * (u + recv))]
        return remote(slot, slot, fz_s.at[d, u], fz_r.at[d, u], z_dev(sign))

    def fz_hop(u):
        def relay(d):
            if u > 0:
                fz_copy(d, u - 1, 1).wait_recv()
            if u < 3 or d == 0:
                fz_copy(d, u).start()
        return relay

    def fx_copy(i, recv=0):
        sign = -1 if i == 1 else 1
        slot = fx.at[lax.rem(x + ((-sign * recv - (i == 2)) % XN), XN)]
        return remote(slot, slot, fx_s.at[i], fx_r.at[i], x_dev(sign))

    def fy_copy(i, recv=0):
        sign = -1 if i == 1 else 1
        slot = fy.at[lax.rem(y + ((-sign * recv - (i == 2)) % YN), YN)]
        return remote(slot, slot, fy_s.at[i], fy_r.at[i], y_dev(sign))

    d_wait(4, 3, 5)
    c_tick(0)
    c_tick(1)
    d_wait(2, 6, 1, 7, 0)
    lax.fori_loop(0, ZN, in_piece, 0)
    acc_in[...] = jnp.dot(hot_c[...], in_terms[...], preferred_element_type=F32)[:8]
    in_swap.start()
    pa_wait(6)
    pre_pair(-2, True)
    pa_wait(3)
    pre_pair(3, True)
    in_swap.wait_recv()
    fz[z] = acc_in[:, my_half] + acc_in_rx[:, my_half]
    c_tick(2, fz_hop(0))
    pa_wait(4, 5)
    pre_pair(-3, True)
    pre_pair(4, True)

    def late_term(i, carry):
        two = rows(2 * lax.rem(z + i + ZN - 1, ZN), 0, 2 * ROWS)
        terms[two] = (C[two].astype(F32) * terms[two].astype(F32)).astype(BF16)
        return carry
    lax.fori_loop(0, 4, late_term, 0)
    c_tick(3, fz_hop(1))
    fx[x] = jnp.dot(hot[:16], terms[...], preferred_element_type=F32)[:8]
    fx_copy(0).start()
    fx_copy(1).start()
    wg_piece(0)
    c_tick(4, fz_hop(2))
    fx_copy(0, 1).wait_recv()
    fx_copy(2).start()
    wg_piece(1)
    fx_copy(1, 1).wait_recv()
    fx_copy(2, 1).wait_recv()
    fy[y] = ((fx[0] + fx[1]) + fx[2]) + fx[3]
    fy_copy(0).start()
    fy_copy(1).start()
    c_tick(5, fz_hop(3))
    wg_piece(2)
    fy_copy(0, 1).wait_recv()
    fy_copy(2).start()
    c_tick(6)
    r_own[...] = member_rows([col], sc_in)
    wg_piece(3)
    fz_copy(0, 3, 1).wait_recv()
    total_in = fz[0]
    for k in range(1, ZN):
        total_in += fz[k]
    fin[:, my_half] = total_in
    half_swap.start()
    fy_copy(1, 1).wait_recv()
    fy_copy(2, 1).wait_recv()
    fout[...] = ((fy[0] + fy[1]) + fy[2]) + fy[3]
    half_back.wait_recv()

    for d in both:
        c_copy(d, 5).wait_recv()
    for d in both:
        c_copy(d, 6).wait_recv()
    for half in both:
        part = pl.ds(HALF * half, HALF)
        total = chip_sum(0, half, HALF)
        total += rb[0, 6 - half].astype(F32) + rb[1, 5 + half].astype(F32)
        ig_v[part] = (total * r_own[part]).astype(BF16)

    for d in both:
        for u in range(7):
            a_copy(d, u).wait_send()
            c_copy(d, u).wait_send()
    for k in range(ZN):
        pa_copy(k).wait_send()
        d_copy(k).wait_send()
    for h in both:
        for d in both:
            b_copy(h, "first", d).wait_send()
            b_copy(h, "first_q", d).wait_send()
            for s in range(4):
                b_copy(h, "second", d, s).wait_send()
                b_copy(h, "second_q", d, s).wait_send()
    in_swap.wait_send()
    half_swap.wait_send()
    for u in range(3):
        fx_copy(u).wait_send()
        fy_copy(u).wait_send()
        for d in both:
            fz_copy(d, u).wait_send()
    fz_copy(0, 3).wait_send()


def local(inputs, weight, cotangent, scale_in, scale_out, member):
    depth, width = weight.shape
    batch = BLOCKS * ROWS
    in_hbm = pl.BlockSpec(memory_space=pltpu.HBM)
    dma = pltpu.SemaphoreType.DMA
    return pl.pallas_call(
        kernel,
        out_shape=(
            pltpu.VMEM((ROWS, depth), BF16),
            pltpu.VMEM((depth, width), F32),
            pltpu.VMEM((8, depth), F32),
            pltpu.VMEM((8, width), F32),
        ),
        in_specs=[in_hbm] * 6,
        out_specs=(pl.BlockSpec(memory_space=pltpu.VMEM),) * 4,
        scratch_shapes=[
            pltpu.VMEM((batch, depth), BF16),
            pltpu.VMEM((batch, width), BF16),
            pltpu.VMEM((batch, depth), BF16),
            pltpu.VMEM((batch, width), BF16),
            pltpu.VMEM((depth, width), BF16),
            pltpu.VMEM((width, depth), BF16),
            pltpu.VMEM((batch, depth), BF16),
            pltpu.VMEM((batch // 2, depth), BF16),
            pltpu.VMEM((2, 7, HALF, depth), BF16),
            pltpu.VMEM((2, 7, HALF, depth), BF16),
            pltpu.VMEM((ROWS, depth), F32),
            pltpu.VMEM((8, depth), F32),
            pltpu.VMEM((8, width), F32),
            pltpu.VMEM((BLOCKS, ROWS), jnp.int32),
            pltpu.VMEM((32, depth), BF16),
            pltpu.VMEM((32, width), BF16),
            pltpu.VMEM((32, batch), BF16),
            pltpu.VMEM((16, batch // 2), BF16),
            pltpu.VMEM((batch, width), BF16),
            pltpu.VMEM((batch // 2, depth), BF16),
            pltpu.VMEM((8, depth), F32),
            pltpu.VMEM((8, depth), F32),
            pltpu.VMEM((ZN, 8, depth // 2), F32),
            pltpu.VMEM((XN, 8, width), F32),
            pltpu.VMEM((YN, 8, width), F32),
            dma((6,)),
            dma((2, 7)), dma((2, 7)), dma((8,)), dma((8,)),
            dma((2, 20)), dma((2, 20)), dma((8,)), dma((8,)),
            dma((2, 7)), dma((2, 7)),
            dma((1,)), dma((1,)), dma((2, 4)), dma((2, 4)),
            dma((1,)), dma((1,)), dma((3,)), dma((3,)), dma((3,)), dma((3,)),
        ],
        compiler_params=pltpu.CompilerParams(
            collective_id=0, has_side_effects=True, vmem_limit_bytes=62500000
        ),
    )(inputs, weight, cotangent, scale_in, scale_out, member.reshape(BLOCKS, ROWS))


def solution(mesh):
    placed = (
        P("col", "row"),
        P("row", "col"),
        P("row", "col"),
        P(None, "row"),
        P(None, "col"),
        P(),
    )
    return jax.shard_map(
        local,
        mesh=mesh,
        in_specs=placed,
        out_specs=(P("col", "row"), P("row", "col"), P(None, "row"), P(None, "col")),
        check_vma=False,
    )
```

time: 83.4 us -> 65.3 us (0.78)
  Pallas kernels: 74.9 us -> 60.6 us
  local copies, waits for them, and re-layouts: 7.7 us -> 3.95 us
    pallas_call x1, Pallas kernels: 74.9 us -> 60.6 us  [local(): pl.pallas_call(kernel, out_shape=(pltpu.VMEM((ROWS, depth), BF16), pltpu....]
    unnamed x8 -> x4, local copies, waits for them, and re-layouts: 7.7 us -> 3.95 us
where the time goes in v2:
time: 65.3 us; the launch traced here: 65.2 us
  Pallas kernels  60.6 us (93%)
  local copies, waits for them, and re-layouts  3.95 us (6%)
    pallas_call x1, Pallas kernels, local(): pl.pallas_call(kernel, out_shape=(pltpu.VMEM((ROWS, depth), BF16), pltpu....  60.6 us
    unnamed x4, local copies, waits for them, and re-layouts  3.95 us

profile of v2, /device:TPU:1, one launch (start us, length us, event | category | flops | bytes accessed | tf_op | source)
XLA Modules:
  0.0 65.2 jit_solution(852765949215045936)
XLA Ops:
  0.6 60.6 %shard_map.93 = (bf16[128,1024]{1,0:T(8,128)(2,1)S(1)}, f32[1024,1024]{1,0:T(8,128)S(1)}, f32[8,1024]{1,0:T(8,128)S(1)}, f32[8,1024]{1,0:T(8,128)S(1)}) custom-call(bf16[128,1024]{1,0:T(8,128)(2,1)} %x_hbm.1, bf16[1024,1024]{1,0:T(8,128)(2,1)} %w_hbm.1, bf16[128,1024]{1,0:T(8,128)(2,1)} %cot_hbm.1, f32[8,1024]{1,0:T(8,128)} %sin_hbm.1, f32[8,1024]{1,0:T(8,128)} %sout_hbm.1, ...), custom_call_target="tpu_custom_call" | custom-call | tf_op jit(solution)/shard_map/pallas_call | solution.py:443
  61.2 0.7 %copy.14 = bf16[128,1024]{1,0:T(8,128)(2,1)} copy(bf16[128,1024]{1,0:T(8,128)(2,1)S(1)} %get-tuple-element.4) | data formatting | bytes 524288
  61.9 0.6 copy.16
  62.6 0.6 copy.17
  63.2 2.0 %copy.15 = f32[1024,1024]{1,0:T(8,128)} copy(f32[1024,1024]{1,0:T(8,128)S(1)} %get-tuple-element.5) | data formatting | bytes 8388608

commit v3 on v0

v3 whole, which is shorter than its diff:
```python
import jax
import jax.numpy as jnp
from jax import lax
from jax.experimental import pallas as pl
from jax.experimental.pallas import tpu as pltpu
from jax.sharding import PartitionSpec as P

MESH = pl.DeviceIdType.MESH
BF16 = jnp.bfloat16
F32 = jnp.float32
XN, YN, ZN = 4, 4, 8
ROWS = 128
HALF = 64
PHASES = 2
STEP = 32
BLOCKS = 16
TN = (((0,), (0,)), ((), ()))


def kernel(
    x_hbm, w_hbm, cot_hbm, sin_hbm, sout_hbm, mem_hbm,
    ig_v, wgs, fin, fout,
    X, C, Xs, Cs, W, WT, pall, prx, sb, rb, r_own,
    sin_v, sout_v, mem_v, sc_in, sc_out,
    hot, hot_rows, terms, in_terms, swap_out, swap_in, fz, fx, fy,
    load_sem,
    a_s, a_r, pa_s, pa_r, b_s, b_r, d_s, d_r, c_s, c_r,
    fp_s, fp_r, fz_s, fz_r, fx_s, fx_r, fy_s, fy_r,
):
    row, col = lax.axis_index("row"), lax.axis_index("col")
    x, y = lax.div(row, YN), lax.rem(row, YN)
    z, c = lax.div(col, 2), lax.rem(col, 2)
    depth, width = W.shape
    both = (0, 1)
    hd = [(h, d) for h in both for d in both]

    def zi(k):
        return lax.rem(z + (k % ZN), ZN)

    def at(dx, dy):
        return YN * lax.rem(x + dx, XN) + lax.rem(y + dy, YN)

    def z_dev(k):
        return (row, 2 * zi(k) + c)

    partner = (row, 2 * z + 1 - c)

    def x_dev(k):
        return (at(k % XN, 0), col)

    def y_dev(k):
        return (at(0, k % YN), col)

    def rows(block, offset=0, size=ROWS):
        return pl.ds(pl.multiple_of(block * ROWS + offset, 16), size)

    def lanes(block):
        return pl.ds(pl.multiple_of(block * ROWS, ROWS), ROWS)

    def remote(src, dst, send, recv, dev):
        return pltpu.make_async_remote_copy(
            src_ref=src, dst_ref=dst, send_sem=send, recv_sem=recv,
            device_id=dev, device_id_type=MESH,
        )

    def a_copy(u, d, recv=0):
        sign = 1 - 2 * d
        block = 2 * zi(-sign * (u // 2 + recv)) + c
        half = u % 2 if d == 0 else 1 - u % 2
        part = X.at[rows(block, HALF * half, HALF)]
        return remote(part, part, a_s.at[d, u], a_r.at[d, u], z_dev(sign))

    def pa_copy(k, recv=0):
        part = X.at[rows(2 * zi(k) + ((1 - c) if recv else c))]
        return remote(part, part, pa_s.at[k], pa_r.at[k], partner)

    def b_block(h, da, db):
        da, db = da % 4, db % 4
        return at(da, db) if h == 0 else at(db, da)

    def b_dev(h, axis, sign):
        along_x = (axis == 0) == (h == 0)
        return x_dev(sign) if along_x else y_dev(sign)

    OFF = (0, -1, 1, 2)

    def b_copy(p, kind, s, h, d, recv=0):
        sign = 1 - 2 * d
        far = 1 if kind in ("first_q", "second_q") else 0
        off, size = (STEP // 2 * d, STEP // 2) if far else (0, STEP)
        if kind in ("first", "first_q"):
            index, block, axis = 2 * far + d, b_block(h, -sign * (far + recv), 0), 0
        else:
            index = 4 + 8 * far + 2 * s + d
            block, axis = b_block(h, OFF[s], -sign * (far + recv)), 1
        part = C.at[rows(block, HALF * p + STEP * h + off, size)]
        return remote(part, part, b_s.at[p, h, index], b_r.at[p, h, index], b_dev(h, axis, sign))

    def d_copy(p, pair, recv=0):
        src = pall.at[rows(2 * pair + (c if recv else (1 - c)), HALF * p, HALF)]
        return remote(src, prx.at[rows(pair, HALF * p, HALF)], d_s.at[p, pair], d_r.at[p, pair], partner)

    def c_copy(p, u, d):
        return remote(sb.at[p, d, u], rb.at[p, d, u], c_s.at[p, d, u], c_r.at[p, d, u], z_dev(1 - 2 * d))

    def fz_copy(u, d, recv=0):
        sign = 1 - 2 * d
        slot = fz.at[zi(-sign * (u + recv))]
        return remote(slot, slot, fz_s.at[d, u], fz_r.at[d, u], z_dev(sign))

    def fx_copy(i, recv=0):
        sign = -1 if i == 1 else 1
        slot = fx.at[lax.rem(x + ((-sign * recv - (i == 2)) % XN), XN)]
        return remote(slot, slot, fx_s.at[i], fx_r.at[i], x_dev(sign))

    def fy_copy(i, recv=0):
        sign = -1 if i == 1 else 1
        slot = fy.at[lax.rem(y + ((-sign * recv - (i == 2)) % YN), YN)]
        return remote(slot, slot, fy_s.at[i], fy_r.at[i], y_dev(sign))

    swap = remote(swap_out, swap_in, fp_s.at[0], fp_r.at[0], partner)

    waited = set()

    def need(name, *key):
        if (name, *key) in waited:
            return
        waited.add((name, *key))
        if name == "a":
            for d in both:
                a_copy(*key, d, 1).wait_recv()
        elif name == "pa":
            pa_copy(*key, 1).wait_recv()
        elif name == "b":
            for h, d in hd:
                b_copy(*key, h, d, 1).wait_recv()
        elif name == "d":
            d_copy(key[0], zi(key[1]), 1).wait_recv()
        elif name == "c":
            for d in both:
                c_copy(*key, d).wait_recv()
        elif name == "fz":
            fz_copy(*key, 1).wait_recv()
        elif name == "fx":
            fx_copy(*key, 1).wait_recv()
        elif name == "fy":
            fy_copy(*key, 1).wait_recv()

    def make_hot(i, carry):
        members = mem_v[pl.ds(i, 1), :]
        ids = lax.broadcasted_iota(jnp.int32, (ROWS, ROWS), 0)
        hit = (lax.rem(ids, 8) == members) & (ids < 24)
        ones = jnp.where(hit, 1.0, 0.0)
        hot[:, lanes(i)] = ones[:16].astype(BF16)
        hot_rows[rows(i)] = ones.T.astype(BF16)
        return carry

    def split(v, out):
        s = v[...]
        hi = s.astype(BF16).astype(F32)
        mid = (s - hi).astype(BF16).astype(F32)
        low = s - hi - mid
        out[...] = jnp.concatenate([hi, mid, low, jnp.zeros_like(s)], axis=0).astype(BF16)

    def stack(parts):
        return parts[0] if len(parts) == 1 else jnp.concatenate(parts, axis=0)

    def scale(parts, size, src, sc, dst):
        ones = stack([hot_rows[part, :32] for part in parts])
        factor = jnp.dot(ones, sc[...], preferred_element_type=F32)
        for i, part in enumerate(parts):
            dst[part] = (src[part].astype(F32) * factor[size * i : size * (i + 1)]).astype(BF16)

    def back(p, *places):
        blocks = [at(dx, dy) for dx, dy in places]
        parts = [rows(block, HALF * p, HALF) for block in blocks]
        scale(parts, HALF, C, sc_out, Cs)
        lhs = stack([Cs[part] for part in parts])
        for n in range(depth // 256):
            cols = pl.ds(256 * n, 256)
            product = jnp.dot(lhs, WT[:, cols], preferred_element_type=F32).astype(BF16)
            for i, part in enumerate(parts):
                pall[part, cols] = product[HALF * i : HALF * (i + 1)]
        for block in blocks:
            @pl.when(lax.rem(block, 2) != c)
            def _():
                d_copy(p, lax.div(block, 2)).start()

    def chip_sum(p, k, half):
        pair, off = zi(k), HALF * p + STEP * half
        own = pall[rows(2 * pair + c, off, STEP)].astype(F32)
        return own + prx[rows(pair, off, STEP)].astype(F32)

    loads = [
        pltpu.make_async_copy(x_hbm, X.at[rows(col)], load_sem.at[0]),
        pltpu.make_async_copy(cot_hbm, C.at[rows(row)], load_sem.at[1]),
        pltpu.make_async_copy(w_hbm, W, load_sem.at[2]),
        pltpu.make_async_copy(sin_hbm, sin_v, load_sem.at[3]),
        pltpu.make_async_copy(sout_hbm, sout_v, load_sem.at[4]),
        pltpu.make_async_copy(mem_hbm, mem_v, load_sem.at[5]),
    ]
    for load in loads:
        load.start()
    barrier = pltpu.get_barrier_semaphore()
    for dev in (z_dev(1), z_dev(-1), x_dev(1), x_dev(-1), y_dev(1), y_dev(-1), partner):
        pl.semaphore_signal(barrier, inc=1, device_id=dev, device_id_type=MESH)
    pl.semaphore_wait(barrier, 7)

    def b_send(p, kind, s=0):
        for h, d in hd:
            b_copy(p, kind, s, h, d).start()

    def b0(p):
        b_send(p, "first")

    def b00(p):
        b_send(p, "second", 0)

    def b1(p):
        need("b", p, "first", 0)
        b_send(p, "first_q")
        b_send(p, "second", 1)
        b_send(p, "second", 2)

    def b2(p):
        need("b", p, "second", 0)
        b_send(p, "second_q", 0)

    def b3(p):
        need("b", p, "first_q", 0)
        b_send(p, "second", 3)

    def b4(p):
        for s in (1, 2):
            need("b", p, "second", s)
            b_send(p, "second_q", s)

    def b5(p):
        need("b", p, "second", 3)
        b_send(p, "second_q", 3)

    def a(u):
        need("a", u)
        if u < 5:
            for d in both:
                a_copy(u + 2, d).start()
        for k in {1: (1, 7), 3: (2, 6), 5: (3, 5), 6: (4,)}.get(u, ()):
            pa_copy(k).start()

    def nbr(p):
        need("b", p, "first", 0)
        need("b", p, "second", 0)
        back(p, (1, 0), (3, 0), (0, 1), (0, 3))

    def diag(p):
        need("b", p, "second", 1)
        need("b", p, "second", 2)
        back(p, (1, 1), (1, 3), (3, 1), (3, 3))

    def anti(p):
        need("b", p, "first_q", 0)
        need("b", p, "second_q", 0)
        back(p, (2, 0), (0, 2))

    def knight(p):
        need("b", p, "second", 3)
        need("b", p, "second_q", 1)
        need("b", p, "second_q", 2)
        back(p, (2, 1), (2, 3), (1, 2), (3, 2))

    def far(p):
        need("b", p, "second_q", 3)
        back(p, (2, 2))

    landed = []

    def pre(k):
        need("pa", k)
        pair = zi(k)
        scale([rows(2 * pair), rows(2 * pair + 1)], ROWS, X, sc_in, Xs)
        two = rows(2 * pair, 0, 2 * ROWS)
        lhs = Xs[two]
        if all(("b", p, "second_q", 3) in waited for p in range(PHASES)):
            landed.append(k)
        for n in range(width // 256):
            cols = pl.ds(256 * n, 256)
            out = jnp.dot(lhs, W[:, cols], preferred_element_type=F32)
            if k in landed:
                out = C[two, cols].astype(F32) * out
            terms[two, cols] = out.astype(BF16)

    def late():
        for k in range(ZN):
            if k not in landed:
                two = rows(2 * zi(k), 0, 2 * ROWS)
                terms[two] = (C[two].astype(F32) * terms[two].astype(F32)).astype(BF16)

    def inx(p):
        def one(i, carry):
            for j in both:
                part = rows(2 * i + j, HALF * p, HALF)
                in_terms[part] = (X[part].astype(F32) * pall[part].astype(F32)).astype(BF16)
            return carry
        for k in range(ZN):
            need("pa", k)
        lax.fori_loop(0, ZN, one, 0)

    def cc(p, u):
        k = 4 - (u + 1) // 2
        for m in (k, -k % ZN):
            need("d", p, m)
        if u >= 2:
            need("c", p, u - 2)
        for d in both:
            half = u % 2 if d == 0 else 1 - u % 2
            total = chip_sum(p, k if d == 0 else -k, half)
            if u >= 2:
                total += rb[p, d, u - 2].astype(F32)
            sb[p, d, u] = total.astype(BF16)
            c_copy(p, u, d).start()

    def fin_rows(p):
        need("d", p, 0)
        need("c", p, 5)
        need("c", p, 6)
        for half in both:
            part = pl.ds(HALF * p + STEP * half, STEP)
            total = chip_sum(p, 0, half)
            total += rb[p, 0, 6 - half].astype(F32) + rb[p, 1, 5 + half].astype(F32)
            ig_v[part] = (total * r_own[part]).astype(BF16)

    def f(i):
        if i == 0:
            partial = jnp.dot(hot[...], in_terms[...], preferred_element_type=F32)
            fz[z] = partial[:8].astype(BF16)
        if 0 < i < 4:
            for d in both:
                need("fz", i - 1, d)
        if i < 4:
            for d in both:
                if i < 3 or d == 0:
                    fz_copy(i, d).start()
        if i == 4:
            need("fz", 3, 0)
            total = fz[0].astype(F32)
            for k in range(1, ZN):
                total += fz[k].astype(F32)
            swap_out[...] = total
            swap.start()
        if i == 5:
            swap.wait_recv()
            fin[...] = swap_out[...] + swap_in[...]

    def o(i):
        if i == 0:
            fx[x] = jnp.dot(hot[...], terms[...], preferred_element_type=F32)[:8]
            fx_copy(0).start()
            fx_copy(1).start()
        if i == 1:
            need("fx", 0)
            fx_copy(2).start()
        if i == 2:
            need("fx", 1)
            need("fx", 2)
            fy[y] = ((fx[0] + fx[1]) + fx[2]) + fx[3]
            fy_copy(0).start()
            fy_copy(1).start()
        if i == 3:
            need("fy", 0)
            fy_copy(2).start()
        if i == 4:
            need("fy", 1)
            need("fy", 2)
            fout[...] = ((fy[0] + fy[1]) + fy[2]) + fy[3]

    def wg(i):
        cols = pl.ds(256 * i, 256)
        for n in range(width // 256):
            wgs[cols, pl.ds(256 * n, 256)] = lax.dot_general(
                Xs[:, cols], Cs[:, pl.ds(256 * n, 256)], TN, preferred_element_type=F32
            )

    def setup():
        for load in loads[2:]:
            load.wait()
        split(sin_v, sc_in)
        split(sout_v, sc_out)
        lax.fori_loop(0, BLOCKS, make_hot, 0)

        def transpose_step(i, carry):
            src = pl.ds(pl.multiple_of(i * 128, 128), 128)
            for k in range(width // 256):
                WT[pl.ds(256 * k, 256), src] = W[src, pl.ds(256 * k, 256)].T
            return carry
        lax.fori_loop(0, depth // 128, transpose_step, 0)
        r_own[...] = jnp.dot(hot_rows[rows(col), :32], sc_in[...], preferred_element_type=F32)
        back(0, (0, 0))
        back(1, (0, 0))

    loads[1].wait()
    b_send(0, "first")
    loads[0].wait()
    for u in (0, 1):
        for d in both:
            a_copy(u, d).start()
    b_send(0, "second", 0)
    pa_copy(0).start()
    setup()
    b0(1)
    b1(0)
    a(0)
    pre(0)
    nbr(0)
    b2(0)
    b3(0)
    a(1)
    b00(1)
    pre(1)
    b4(0)
    a(2)
    diag(0)
    b5(0)
    b1(1)
    anti(0)
    a(3)
    b2(1)
    nbr(1)
    knight(0)
    a(4)
    far(0)
    pre(6)
    b3(1)
    pre(7)
    cc(0, 0)
    a(5)
    b4(1)
    diag(1)
    cc(0, 1)
    anti(1)
    pre(5)
    a(6)
    b5(1)
    pre(2)
    cc(0, 2)
    knight(1)
    inx(0)
    cc(0, 3)
    far(1)
    inx(1)
    f(0)
    cc(1, 0)
    pre(4)
    cc(1, 1)
    cc(0, 4)
    pre(3)
    late()
    o(0)
    f(1)
    cc(1, 2)
    wg(3)
    cc(1, 3)
    o(1)
    cc(0, 5)
    wg(1)
    f(2)
    cc(1, 4)
    wg(0)
    cc(1, 5)
    o(2)
    f(3)
    cc(0, 6)
    cc(1, 6)
    o(3)
    f(4)
    wg(2)
    f(5)
    fin_rows(0)
    o(4)
    fin_rows(1)
    for d in both:
        for u in range(7):
            a_copy(u, d).wait_send()
            for p in range(PHASES):
                c_copy(p, u, d).wait_send()
        for u in range(3):
            fz_copy(u, d).wait_send()
    fz_copy(3, 0).wait_send()
    for k in range(ZN):
        pa_copy(k).wait_send()
        for p in range(PHASES):
            d_copy(p, k).wait_send()
    for p in range(PHASES):
        for h, d in hd:
            for kind in ("first", "first_q"):
                b_copy(p, kind, 0, h, d).wait_send()
            for kind in ("second", "second_q"):
                for s in range(4):
                    b_copy(p, kind, s, h, d).wait_send()
    for u in range(3):
        fx_copy(u).wait_send()
        fy_copy(u).wait_send()
    swap.wait_send()


def write_out(*refs):
    sems = refs[-1]
    ig_v, wg_v, fin_v, fout_v, ig_o, wg_o, fin_o, fout_o = refs[:-1]
    copies = []
    depth = wg_v.shape[0]
    parts = [(ig_v, ig_o), (fin_v, fin_o), (fout_v, fout_o)]
    for i in range(4):
        part = pl.ds(depth // 4 * i, depth // 4)
        parts.append((wg_v.at[part], wg_o.at[part]))
    for i, (src, dst) in enumerate(parts):
        copies.append(pltpu.make_async_copy(src, dst, sems.at[i]))
        copies[-1].start()
    for copy in copies:
        copy.wait()


def local(inputs, weight, cotangent, scale_in, scale_out, member):
    depth, width = weight.shape
    batch = BLOCKS * ROWS
    in_hbm = pl.BlockSpec(memory_space=pltpu.HBM)
    in_vmem = pl.BlockSpec(memory_space=pltpu.VMEM)
    dma = pltpu.SemaphoreType.DMA
    outs = (
        ((ROWS, depth), BF16),
        ((depth, width), F32),
        ((8, depth), F32),
        ((8, width), F32),
    )
    results = pl.pallas_call(
        kernel,
        out_shape=tuple(pltpu.VMEM(*out) for out in outs),
        in_specs=[in_hbm] * 6,
        out_specs=(in_vmem,) * 4,
        scratch_shapes=[
            pltpu.VMEM((batch, depth), BF16),
            pltpu.VMEM((batch, width), BF16),
            pltpu.VMEM((batch, depth), BF16),
            pltpu.VMEM((batch, width), BF16),
            pltpu.VMEM((depth, width), BF16),
            pltpu.VMEM((width, depth), BF16),
            pltpu.VMEM((batch, depth), BF16),
            pltpu.VMEM((batch // 2, depth), BF16),
            pltpu.VMEM((PHASES, 2, 7, STEP, depth), BF16),
            pltpu.VMEM((PHASES, 2, 7, STEP, depth), BF16),
            pltpu.VMEM((ROWS, depth), F32),
            pltpu.VMEM((8, depth), F32),
            pltpu.VMEM((8, width), F32),
            pltpu.VMEM((BLOCKS, ROWS), jnp.int32),
            pltpu.VMEM((32, depth), BF16),
            pltpu.VMEM((32, width), BF16),
            pltpu.VMEM((16, batch), BF16),
            pltpu.VMEM((batch, ROWS), BF16),
            pltpu.VMEM((batch, width), BF16),
            pltpu.VMEM((batch, depth), BF16),
            pltpu.VMEM((8, depth), F32),
            pltpu.VMEM((8, depth), F32),
            pltpu.VMEM((ZN, 8, depth), BF16),
            pltpu.VMEM((XN, 8, width), F32),
            pltpu.VMEM((YN, 8, width), F32),
            dma((6,)),
            dma((2, 7)), dma((2, 7)), dma((8,)), dma((8,)),
            dma((2, 2, 20)), dma((2, 2, 20)), dma((2, 8)), dma((2, 8)),
            dma((2, 2, 7)), dma((2, 2, 7)),
            dma((1,)), dma((1,)), dma((2, 4)), dma((2, 4)),
            dma((3,)), dma((3,)), dma((3,)), dma((3,)),
        ],
        compiler_params=pltpu.CompilerParams(
            collective_id=0, has_side_effects=True, vmem_limit_bytes=62500000
        ),
    )(inputs, weight, cotangent, scale_in, scale_out, member.reshape(BLOCKS, ROWS))
    return pl.pallas_call(
        write_out,
        out_shape=tuple(jax.ShapeDtypeStruct(*out) for out in outs),
        in_specs=[in_vmem] * 4,
        out_specs=(in_hbm,) * 4,
        scratch_shapes=[dma((7,))],
        compiler_params=pltpu.CompilerParams(vmem_limit_bytes=8 * 1024 * 1024),
    )(*results)


def solution(mesh):
    placed = (
        P("col", "row"),
        P("row", "col"),
        P("row", "col"),
        P(None, "row"),
        P(None, "col"),
        P(),
    )
    return jax.shard_map(
        local,
        mesh=mesh,
        in_specs=placed,
        out_specs=(P("col", "row"), P("row", "col"), P(None, "row"), P(None, "col")),
        check_vma=False,
    )
```

time: 196 us -> 62.7 us (0.32); the launches traced: 194 us -> 62.6 us
  waiting for transfers between devices: 99.8 us -> 0 us
  Pallas kernels: 0 us -> 61.8 us
  matrix products: 48.2 us -> 0 us
  blocking collectives: 18.7 us -> 0 us
  between operations: 13.8 us -> 0.8 us
  starting transfers between devices: 6.65 us -> 0 us
  local copies, waits for them, and re-layouts: 3.59 us -> 0 us
  other arithmetic: 3.25 us -> 0 us
    all_gather x2 -> x0, waiting for transfers between devices: 84.8 us -> none  [the longest x1 61.8 us: local(): full_cot = lax.all_gather(cotangent, 'row', axis=0, tiled=True)]
    pallas_call x0 -> x2, Pallas kernels: none -> 61.8 us  [the longest x1 59.6 us: local(): pl.pallas_call(kernel, out_shape=tuple((pltpu.VMEM(*out) for out in outs)...]
    dot_general x7 -> x0, matrix products: 48.2 us -> none  [the longest x1 13 us: local(): lax.dot_general(scaled_in, scaled_cot, (((0,), (0,)), ((), ())), preferre...]
    all_gather x1 -> x0, blocking collectives: 18.7 us -> none  [gathered_total(): return lax.all_gather(value, axis).sum(0)]
    reduce_scatter x1 -> x0, waiting for transfers between devices: 13.6 us -> none  [local(): lax.psum_scatter(back_part, 'col', scatter_dimension=0, tiled=True)]
    all_to_all x1 -> x0, starting transfers between devices: 6.54 us -> none  [from_everyone(): return lax.all_to_all(copies, axis, split_axis=0, concat_axis=0, tiled=True)]
    unnamed x12 -> x0, local copies, waits for them, and re-layouts: 2.71 us -> none
    convert_element_type x1 -> x0, other arithmetic: 1.96 us -> none  [local(): input_grad = (back_block * r_block).astype(jnp.bfloat16)]
  transfers between devices with their start and end apart: 4 -> 0, of which waited for: 3 -> 0; matrix products, arithmetic and copies ran while one was open for 26% -> 0% of each run, Pallas kernels for 0% -> 0%
where the time goes in v3:
time: 62.7 us; the launch traced here: 62.6 us
  Pallas kernels  61.8 us (99%)
  between operations  0.8 us (1%)
    pallas_call x1, Pallas kernels, local(): pl.pallas_call(kernel, out_shape=tuple((pltpu.VMEM(*out) for out in outs)...  59.6 us
    pallas_call x1, Pallas kernels, local(): pl.pallas_call(write_out, out_shape=tuple((jax.ShapeDtypeStruct(*out) for...  2.18 us

profile of v3, /device:TPU:1, one launch (start us, length us, event | category | flops | bytes accessed | tf_op | source)
XLA Modules:
  0.0 62.6 jit_solution(14718651320718219368)
XLA Ops:
  0.6 59.6 %shard_map.93 = (bf16[128,1024]{1,0:T(8,128)(2,1)S(1)}, f32[1024,1024]{1,0:T(8,128)S(1)}, f32[8,1024]{1,0:T(8,128)S(1)}, f32[8,1024]{1,0:T(8,128)S(1)}) custom-call(bf16[128,1024]{1,0:T(8,128)(2,1)} %x_hbm.1, bf16[1024,1024]{1,0:T(8,128)(2,1)} %w_hbm.1, bf16[128,1024]{1,0:T(8,128)(2,1)} %cot_hbm.1, f32[8,1024]{1,0:T(8,128)} %sin_hbm.1, f32[8,1024]{1,0:T(8,128)} %sout_hbm.1, ...), custom_call_target="tpu_custom_call" | custom-call | tf_op jit(solution)/shard_map/pallas_call | solution.py:533
  60.3 2.2 %shard_map.94 = (bf16[128,1024]{1,0:T(8,128)(2,1)}, f32[1024,1024]{1,0:T(8,128)}, f32[8,1024]{1,0:T(8,128)}, f32[8,1024]{1,0:T(8,128)}) custom-call(bf16[128,1024]{1,0:T(8,128)(2,1)S(1)} %get-tuple-element.8.refs_0_, f32[1024,1024]{1,0:T(8,128)S(1)} %get-tuple-element.9.refs_1_, f32[8,1024]{1,0:T(8,128)S(1)} %get-tuple-element.10.refs_2_, ...), custom_call_target="tpu_custom_call" | custom-call | tf_op jit(solution)/shard_map/pallas_call | solution.py:575

commit v4 on v3

--- a/solution.py
+++ b/solution.py
@@ -14,6 +14,7 @@
 PHASES = 2
 STEP = 32
 BLOCKS = 16
+LONG_HOP = {"x": 1, "y": 1, "z": 0}
 TN = (((0,), (0,)), ((), ()))
 
 
@@ -32,12 +33,19 @@
     z, c = lax.div(col, 2), lax.rem(col, 2)
     depth, width = W.shape
     both = (0, 1)
-    hd = [(h, d) for h in both for d in both]
+    place = {"x": x, "y": y, "z": z}
+
+    def way(axis, q):
+        return lax.rem(place[axis] + (q + LONG_HOP[axis]), 2)
+
+    def sign(axis, q):
+        return 1 - 2 * way(axis, q)
 
     def zi(k):
-        return lax.rem(z + (k % ZN), ZN)
+        return lax.rem(z + (k % ZN if isinstance(k, int) else k + ZN), ZN)
 
     def at(dx, dy):
+        dx, dy = (v % 4 if isinstance(v, int) else v + 4 for v in (dx, dy))
         return YN * lax.rem(x + dx, XN) + lax.rem(y + dy, YN)
 
     def z_dev(k):
@@ -46,10 +54,10 @@
     partner = (row, 2 * z + 1 - c)
 
     def x_dev(k):
-        return (at(k % XN, 0), col)
+        return (at(k, 0), col)
 
     def y_dev(k):
-        return (at(0, k % YN), col)
+        return (at(0, k), col)
 
     def rows(block, offset=0, size=ROWS):
         return pl.ds(pl.multiple_of(block * ROWS + offset, 16), size)
@@ -63,50 +71,51 @@
             device_id=dev, device_id_type=MESH,
         )
 
-    def a_copy(u, d, recv=0):
-        sign = 1 - 2 * d
-        block = 2 * zi(-sign * (u // 2 + recv)) + c
-        half = u % 2 if d == 0 else 1 - u % 2
+    def a_copy(u, q, recv=0):
+        d, sg = way("z", q), sign("z", q)
+        block = 2 * zi(-sg * (u // 2 + recv)) + c
+        half = lax.rem(u + d, 2)
         part = X.at[rows(block, HALF * half, HALF)]
-        return remote(part, part, a_s.at[d, u], a_r.at[d, u], z_dev(sign))
+        return remote(part, part, a_s.at[d, u], a_r.at[d, u], z_dev(sg))
 
     def pa_copy(k, recv=0):
         part = X.at[rows(2 * zi(k) + ((1 - c) if recv else c))]
-        return remote(part, part, pa_s.at[k], pa_r.at[k], partner)
+        slot = zi(k)
+        return remote(part, part, pa_s.at[slot], pa_r.at[slot], partner)
+
+    def b_axis(h, axis):
+        return "x" if (axis == 0) == (h == 0) else "y"
 
     def b_block(h, da, db):
-        da, db = da % 4, db % 4
         return at(da, db) if h == 0 else at(db, da)
 
-    def b_dev(h, axis, sign):
-        along_x = (axis == 0) == (h == 0)
-        return x_dev(sign) if along_x else y_dev(sign)
-
-    OFF = (0, -1, 1, 2)
-
-    def b_copy(p, kind, s, h, d, recv=0):
-        sign = 1 - 2 * d
+    def b_copy(p, kind, s, h, q, recv=0):
         far = 1 if kind in ("first_q", "second_q") else 0
+        name = b_axis(h, 0 if kind in ("first", "first_q") else 1)
+        d, sg = way(name, q), sign(name, q)
         off, size = (STEP // 2 * d, STEP // 2) if far else (0, STEP)
-        if kind in ("first", "first_q"):
-            index, block, axis = 2 * far + d, b_block(h, -sign * (far + recv), 0), 0
+        if name == b_axis(h, 0):
+            index, block = 2 * far + d, b_block(h, -sg * (far + recv), 0)
         else:
             index = 4 + 8 * far + 2 * s + d
-            block, axis = b_block(h, OFF[s], -sign * (far + recv)), 1
+            da = -sign(b_axis(h, 0), s - 1) if s in (1, 2) else (0, 0, 0, 2)[s]
+            block = b_block(h, da, -sg * (far + recv))
         part = C.at[rows(block, HALF * p + STEP * h + off, size)]
-        return remote(part, part, b_s.at[p, h, index], b_r.at[p, h, index], b_dev(h, axis, sign))
+        dev = x_dev(sg) if name == "x" else y_dev(sg)
+        return remote(part, part, b_s.at[p, h, index], b_r.at[p, h, index], dev)
 
     def d_copy(p, pair, recv=0):
         src = pall.at[rows(2 * pair + (c if recv else (1 - c)), HALF * p, HALF)]
         return remote(src, prx.at[rows(pair, HALF * p, HALF)], d_s.at[p, pair], d_r.at[p, pair], partner)
 
-    def c_copy(p, u, d):
-        return remote(sb.at[p, d, u], rb.at[p, d, u], c_s.at[p, d, u], c_r.at[p, d, u], z_dev(1 - 2 * d))
-
-    def fz_copy(u, d, recv=0):
-        sign = 1 - 2 * d
-        slot = fz.at[zi(-sign * (u + recv))]
-        return remote(slot, slot, fz_s.at[d, u], fz_r.at[d, u], z_dev(sign))
+    def c_copy(p, u, q):
+        d = way("z", q)
+        return remote(sb.at[p, d, u], rb.at[p, d, u], c_s.at[p, d, u], c_r.at[p, d, u], z_dev(sign("z", q)))
+
+    def fz_copy(u, q, recv=0):
+        d, sg = way("z", q), sign("z", q)
+        slot = fz.at[zi(-sg * (u + recv))]
+        return remote(slot, slot, fz_s.at[d, u], fz_r.at[d, u], z_dev(sg))
 
     def fx_copy(i, recv=0):
         sign = -1 if i == 1 else 1
@@ -121,24 +130,26 @@
     swap = remote(swap_out, swap_in, fp_s.at[0], fp_r.at[0], partner)
 
     waited = set()
+
+    def step_of(j, q=None):
+        return j if q is None else -sign("z", q) * j
 
     def need(name, *key):
         if (name, *key) in waited:
             return
         waited.add((name, *key))
         if name == "a":
-            for d in both:
-                a_copy(*key, d, 1).wait_recv()
+            a_copy(*key, 1).wait_recv()
         elif name == "pa":
-            pa_copy(*key, 1).wait_recv()
+            pa_copy(step_of(*key), 1).wait_recv()
         elif name == "b":
-            for h, d in hd:
-                b_copy(*key, h, d, 1).wait_recv()
+            p, kind, s, q = key
+            for h in both:
+                b_copy(p, kind, s, h, q, 1).wait_recv()
         elif name == "d":
-            d_copy(key[0], zi(key[1]), 1).wait_recv()
+            d_copy(key[0], zi(step_of(*key[1:])), 1).wait_recv()
         elif name == "c":
-            for d in both:
-                c_copy(*key, d).wait_recv()
+            c_copy(*key).wait_recv()
         elif name == "fz":
             fz_copy(*key, 1).wait_recv()
         elif name == "fx":
@@ -206,93 +217,102 @@
         pl.semaphore_signal(barrier, inc=1, device_id=dev, device_id_type=MESH)
     pl.semaphore_wait(barrier, 7)
 
-    def b_send(p, kind, s=0):
-        for h, d in hd:
-            b_copy(p, kind, s, h, d).start()
+    def b_send(p, kind, s, qs=both):
+        for q in qs:
+            for h in both:
+                b_copy(p, kind, s, h, q).start()
+
+    def b_need(p, kind, s):
+        for q in both:
+            need("b", p, kind, s, q)
 
     def b0(p):
-        b_send(p, "first")
+        b_send(p, "first", 0)
 
     def b00(p):
         b_send(p, "second", 0)
 
-    def b1(p):
-        need("b", p, "first", 0)
-        b_send(p, "first_q")
-        b_send(p, "second", 1)
-        b_send(p, "second", 2)
-
-    def b2(p):
-        need("b", p, "second", 0)
-        b_send(p, "second_q", 0)
+    def b1(p, q):
+        need("b", p, "first", 0, q)
+        b_send(p, "first_q", 0, (q,))
+        b_send(p, "second", 1 + q)
+
+    def b2(p, q):
+        need("b", p, "second", 0, q)
+        b_send(p, "second_q", 0, (q,))
 
     def b3(p):
-        need("b", p, "first_q", 0)
+        b_need(p, "first_q", 0)
         b_send(p, "second", 3)
 
-    def b4(p):
+    def b4(p, q):
         for s in (1, 2):
-            need("b", p, "second", s)
-            b_send(p, "second_q", s)
-
-    def b5(p):
-        need("b", p, "second", 3)
-        b_send(p, "second_q", 3)
-
-    def a(u):
-        need("a", u)
+            need("b", p, "second", s, q)
+            b_send(p, "second_q", s, (q,))
+
+    def b5(p, q):
+        need("b", p, "second", 3, q)
+        b_send(p, "second_q", 3, (q,))
+
+    def a(u, q):
+        need("a", u, q)
         if u < 5:
-            for d in both:
-                a_copy(u + 2, d).start()
-        for k in {1: (1, 7), 3: (2, 6), 5: (3, 5), 6: (4,)}.get(u, ()):
-            pa_copy(k).start()
+            a_copy(u + 2, q).start()
+        if u % 2:
+            pa_copy(-sign("z", q) * (u // 2 + 1)).start()
+
+    def a6():
+        need("a", 6, 0)
+        need("a", 6, 1)
+        pa_copy(4).start()
 
     def nbr(p):
-        need("b", p, "first", 0)
-        need("b", p, "second", 0)
+        b_need(p, "first", 0)
+        b_need(p, "second", 0)
         back(p, (1, 0), (3, 0), (0, 1), (0, 3))
 
     def diag(p):
-        need("b", p, "second", 1)
-        need("b", p, "second", 2)
+        b_need(p, "second", 1)
+        b_need(p, "second", 2)
         back(p, (1, 1), (1, 3), (3, 1), (3, 3))
 
     def anti(p):
-        need("b", p, "first_q", 0)
-        need("b", p, "second_q", 0)
+        b_need(p, "first_q", 0)
+        b_need(p, "second_q", 0)
         back(p, (2, 0), (0, 2))
 
     def knight(p):
-        need("b", p, "second", 3)
-        need("b", p, "second_q", 1)
-        need("b", p, "second_q", 2)
+        b_need(p, "second", 3)
+        b_need(p, "second_q", 1)
+        b_need(p, "second_q", 2)
         back(p, (2, 1), (2, 3), (1, 2), (3, 2))
 
     def far(p):
-        need("b", p, "second_q", 3)
+        b_need(p, "second_q", 3)
         back(p, (2, 2))
 
+    all_pairs = [(0,), (4,)] + [(j, q) for j in (1, 2, 3) for q in both]
     landed = []
 
-    def pre(k):
-        need("pa", k)
-        pair = zi(k)
+    def pre(*key):
+        need("pa", *key)
+        pair = zi(step_of(*key))
         scale([rows(2 * pair), rows(2 * pair + 1)], ROWS, X, sc_in, Xs)
         two = rows(2 * pair, 0, 2 * ROWS)
         lhs = Xs[two]
-        if all(("b", p, "second_q", 3) in waited for p in range(PHASES)):
-            landed.append(k)
+        if all(("b", p, "second_q", 3, q) in waited for p in range(PHASES) for q in both):
+            landed.append(key)
         for n in range(width // 256):
             cols = pl.ds(256 * n, 256)
             out = jnp.dot(lhs, W[:, cols], preferred_element_type=F32)
-            if k in landed:
+            if key in landed:
                 out = C[two, cols].astype(F32) * out
             terms[two, cols] = out.astype(BF16)
 
     def late():
-        for k in range(ZN):
-            if k not in landed:
-                two = rows(2 * zi(k), 0, 2 * ROWS)
+        for key in all_pairs:
+            if key not in landed:
+                two = rows(2 * zi(step_of(*key)), 0, 2 * ROWS)
                 terms[two] = (C[two].astype(F32) * terms[two].astype(F32)).astype(BF16)
 
     def inx(p):
@@ -301,47 +321,46 @@
                 part = rows(2 * i + j, HALF * p, HALF)
                 in_terms[part] = (X[part].astype(F32) * pall[part].astype(F32)).astype(BF16)
             return carry
-        for k in range(ZN):
-            need("pa", k)
+        for key in all_pairs:
+            need("pa", *key)
         lax.fori_loop(0, ZN, one, 0)
 
-    def cc(p, u):
+    def cc(p, u, q):
         k = 4 - (u + 1) // 2
-        for m in (k, -k % ZN):
-            need("d", p, m)
+        need("d", p, *((4,) if k == 4 else (k, 1 - q)))
         if u >= 2:
-            need("c", p, u - 2)
-        for d in both:
-            half = u % 2 if d == 0 else 1 - u % 2
-            total = chip_sum(p, k if d == 0 else -k, half)
-            if u >= 2:
-                total += rb[p, d, u - 2].astype(F32)
-            sb[p, d, u] = total.astype(BF16)
-            c_copy(p, u, d).start()
+            need("c", p, u - 2, q)
+        d = way("z", q)
+        total = chip_sum(p, sign("z", q) * k, lax.rem(u + d, 2))
+        if u >= 2:
+            total += rb[p, d, u - 2].astype(F32)
+        sb[p, d, u] = total.astype(BF16)
+        c_copy(p, u, q).start()
 
     def fin_rows(p):
         need("d", p, 0)
-        need("c", p, 5)
-        need("c", p, 6)
+        for u in (5, 6):
+            for q in both:
+                need("c", p, u, q)
         for half in both:
             part = pl.ds(HALF * p + STEP * half, STEP)
             total = chip_sum(p, 0, half)
             total += rb[p, 0, 6 - half].astype(F32) + rb[p, 1, 5 + half].astype(F32)
             ig_v[part] = (total * r_own[part]).astype(BF16)
 
-    def f(i):
+    def f(i, *qs):
         if i == 0:
             partial = jnp.dot(hot[...], in_terms[...], preferred_element_type=F32)
             fz[z] = partial[:8].astype(BF16)
+            fz_copy(0, 0).start()
+            fz_copy(0, 1).start()
         if 0 < i < 4:
-            for d in both:
-                need("fz", i - 1, d)
-        if i < 4:
-            for d in both:
-                if i < 3 or d == 0:
-                    fz_copy(i, d).start()
+            for q in qs or (0,):
+                need("fz", i - 1, q)
+                fz_copy(i, q).start()
         if i == 4:
-            need("fz", 3, 0)
+            need("fz", 2, 1)
+            need("fz", 3, 1)
             total = fz[0].astype(F32)
             for k in range(1, ZN):
                 total += fz[k].astype(F32)
@@ -398,78 +417,108 @@
         back(1, (0, 0))
 
     loads[1].wait()
-    b_send(0, "first")
+    b_send(0, "first", 0)
     loads[0].wait()
     for u in (0, 1):
-        for d in both:
-            a_copy(u, d).start()
+        for q in both:
+            a_copy(u, q).start()
     b_send(0, "second", 0)
     pa_copy(0).start()
     setup()
     b0(1)
-    b1(0)
-    a(0)
+    b1(0, 0)
+    b1(0, 1)
+    a(0, 0)
+    a(0, 1)
     pre(0)
     nbr(0)
-    b2(0)
+    b2(0, 0)
+    b2(0, 1)
     b3(0)
-    a(1)
+    a(1, 0)
+    a(1, 1)
     b00(1)
-    pre(1)
-    b4(0)
-    a(2)
+    pre(1, 0)
+    b4(0, 0)
+    b4(0, 1)
+    a(2, 0)
+    a(2, 1)
     diag(0)
-    b5(0)
-    b1(1)
+    b5(0, 0)
+    b5(0, 1)
+    b1(1, 0)
+    b1(1, 1)
     anti(0)
-    a(3)
-    b2(1)
+    a(3, 0)
+    a(3, 1)
+    b2(1, 0)
+    b2(1, 1)
     nbr(1)
     knight(0)
-    a(4)
+    a(4, 0)
+    a(4, 1)
     far(0)
-    pre(6)
+    pre(2, 1)
     b3(1)
-    pre(7)
-    cc(0, 0)
-    a(5)
-    b4(1)
+    pre(1, 1)
+    cc(0, 0, 0)
+    cc(0, 0, 1)
+    a(5, 0)
+    a(5, 1)
+    b4(1, 0)
+    b4(1, 1)
     diag(1)
-    cc(0, 1)
+    cc(0, 1, 0)
+    cc(0, 1, 1)
     anti(1)
-    pre(5)
-    a(6)
-    b5(1)
-    pre(2)
-    cc(0, 2)
+    pre(3, 1)
+    a6()
+    b5(1, 0)
+    b5(1, 1)
+    pre(2, 0)
+    cc(0, 2, 0)
+    cc(0, 2, 1)
     knight(1)
     inx(0)
-    cc(0, 3)
+    cc(0, 3, 0)
+    cc(0, 3, 1)
     far(1)
     inx(1)
     f(0)
-    cc(1, 0)
+    cc(1, 0, 0)
+    cc(1, 0, 1)
     pre(4)
-    cc(1, 1)
-    cc(0, 4)
-    pre(3)
+    cc(1, 1, 0)
+    cc(1, 1, 1)
+    cc(0, 4, 0)
+    cc(0, 4, 1)
+    pre(3, 0)
     late()
     o(0)
-    f(1)
-    cc(1, 2)
+    f(1, 0)
+    f(1, 1)
+    cc(1, 2, 0)
+    cc(1, 2, 1)
     wg(3)
-    cc(1, 3)
+    cc(1, 3, 0)
+    cc(1, 3, 1)
     o(1)
-    cc(0, 5)
+    cc(0, 5, 0)
+    cc(0, 5, 1)
     wg(1)
-    f(2)
-    cc(1, 4)
+    f(2, 0)
+    f(2, 1)
+    cc(1, 4, 0)
+    cc(1, 4, 1)
     wg(0)
-    cc(1, 5)
+    cc(1, 5, 0)
+    cc(1, 5, 1)
     o(2)
     f(3)
-    cc(0, 6)
-    cc(1, 6)
+    cc(0, 6, 0)
+    cc(0, 6, 1)
+    cc(1, 6, 0)
+    cc(1, 6, 1)
     o(3)
     f(4)
     wg(2)
@@ -477,25 +526,26 @@
     fin_rows(0)
     o(4)
     fin_rows(1)
-    for d in both:
+    for q in both:
         for u in range(7):
-            a_copy(u, d).wait_send()
+            a_copy(u, q).wait_send()
             for p in range(PHASES):
-                c_copy(p, u, d).wait_send()
+                c_copy(p, u, q).wait_send()
         for u in range(3):
-            fz_copy(u, d).wait_send()
+            fz_copy(u, q).wait_send()
     fz_copy(3, 0).wait_send()
     for k in range(ZN):
         pa_copy(k).wait_send()
         for p in range(PHASES):
             d_copy(p, k).wait_send()
     for p in range(PHASES):
-        for h, d in hd:
-            for kind in ("first", "first_q"):
-                b_copy(p, kind, 0, h, d).wait_send()
-            for kind in ("second", "second_q"):
-                for s in range(4):
-                    b_copy(p, kind, s, h, d).wait_send()
+        for h in both:
+            for q in both:
+                for kind in ("first", "first_q"):
+                    b_copy(p, kind, 0, h, q).wait_send()
+                for kind in ("second", "second_q"):
+                    for s in range(4):
+                        b_copy(p, kind, s, h, q).wait_send()
     for u in range(3):
         fx_copy(u).wait_send()
         fy_copy(u).wait_send()

time: 62.7 us -> 61.4 us (0.979)
  Pallas kernels: 61.8 us -> 60 us
    pallas_call x1, Pallas kernels: 59.6 us -> 57.8 us  [local(): pl.pallas_call(kernel, out_shape=tuple((pltpu.VMEM(*out) for out in outs)...]
where the time goes in v4:
time: 61.4 us; the launch traced here: 60.8 us
  Pallas kernels  60 us (98%)
  between operations  0.8 us (1%)
    pallas_call x1, Pallas kernels, local(): pl.pallas_call(kernel, out_shape=tuple((pltpu.VMEM(*out) for out in outs)...  57.8 us
    pallas_call x1, Pallas kernels, local(): pl.pallas_call(write_out, out_shape=tuple((jax.ShapeDtypeStruct(*out) for...  2.18 us

profile of v4, /device:TPU:1, one launch (start us, length us, event | category | flops | bytes accessed | tf_op | source)
XLA Modules:
  0.0 60.8 jit_solution(8667779712074186351)
XLA Ops:
  0.6 57.8 %shard_map.93 = (bf16[128,1024]{1,0:T(8,128)(2,1)S(1)}, f32[1024,1024]{1,0:T(8,128)S(1)}, f32[8,1024]{1,0:T(8,128)S(1)}, f32[8,1024]{1,0:T(8,128)S(1)}) custom-call(bf16[128,1024]{1,0:T(8,128)(2,1)} %x_hbm.1, bf16[1024,1024]{1,0:T(8,128)(2,1)} %w_hbm.1, bf16[128,1024]{1,0:T(8,128)(2,1)} %cot_hbm.1, f32[8,1024]{1,0:T(8,128)} %sin_hbm.1, f32[8,1024]{1,0:T(8,128)} %sout_hbm.1, ...), custom_call_target="tpu_custom_call" | custom-call | tf_op jit(solution)/shard_map/pallas_call | solution.py:583
  58.5 2.2 %shard_map.94 = (bf16[128,1024]{1,0:T(8,128)(2,1)}, f32[1024,1024]{1,0:T(8,128)}, f32[8,1024]{1,0:T(8,128)}, f32[8,1024]{1,0:T(8,128)}) custom-call(bf16[128,1024]{1,0:T(8,128)(2,1)S(1)} %get-tuple-element.8.refs_0_, f32[1024,1024]{1,0:T(8,128)S(1)} %get-tuple-element.9.refs_1_, f32[8,1024]{1,0:T(8,128)S(1)} %get-tuple-element.10.refs_2_, ...), custom_call_target="tpu_custom_call" | custom-call | tf_op jit(solution)/shard_map/pallas_call | solution.py:625

commit v5 on v4

--- a/solution.py
+++ b/solution.py
@@ -413,8 +413,6 @@
             return carry
         lax.fori_loop(0, depth // 128, transpose_step, 0)
         r_own[...] = jnp.dot(hot_rows[rows(col), :32], sc_in[...], preferred_element_type=F32)
-        back(0, (0, 0))
-        back(1, (0, 0))
 
     loads[1].wait()
     b_send(0, "first", 0)
@@ -430,6 +428,8 @@
     b1(0, 1)
     a(0, 0)
     a(0, 1)
+    back(0, (0, 0))
+    back(1, (0, 0))
     pre(0)
     nbr(0)
     b2(0, 0)

time: 61.4 us -> 60.5 us (0.985)
  no operation moved by 1% of the time
where the time goes in v5:
time: 60.5 us; the launch traced here: 60.2 us
  Pallas kernels  59.4 us (98%)
  between operations  0.8 us (1%)
    pallas_call x1, Pallas kernels, local(): pl.pallas_call(kernel, out_shape=tuple((pltpu.VMEM(*out) for out in outs)...  57.2 us
    pallas_call x1, Pallas kernels, local(): pl.pallas_call(write_out, out_shape=tuple((jax.ShapeDtypeStruct(*out) for...  2.18 us

profile of v5, /device:TPU:1, one launch (start us, length us, event | category | flops | bytes accessed | tf_op | source)
XLA Modules:
  0.0 60.2 jit_solution(16109697345605715979)
XLA Ops:
  0.6 57.2 %shard_map.93 = (bf16[128,1024]{1,0:T(8,128)(2,1)S(1)}, f32[1024,1024]{1,0:T(8,128)S(1)}, f32[8,1024]{1,0:T(8,128)S(1)}, f32[8,1024]{1,0:T(8,128)S(1)}) custom-call(bf16[128,1024]{1,0:T(8,128)(2,1)} %x_hbm.1, bf16[1024,1024]{1,0:T(8,128)(2,1)} %w_hbm.1, bf16[128,1024]{1,0:T(8,128)(2,1)} %cot_hbm.1, f32[8,1024]{1,0:T(8,128)} %sin_hbm.1, f32[8,1024]{1,0:T(8,128)} %sout_hbm.1, ...), custom_call_target="tpu_custom_call" | custom-call | tf_op jit(solution)/shard_map/pallas_call | solution.py:583
  57.9 2.2 %shard_map.94 = (bf16[128,1024]{1,0:T(8,128)(2,1)}, f32[1024,1024]{1,0:T(8,128)}, f32[8,1024]{1,0:T(8,128)}, f32[8,1024]{1,0:T(8,128)}) custom-call(bf16[128,1024]{1,0:T(8,128)(2,1)S(1)} %get-tuple-element.8.refs_0_, f32[1024,1024]{1,0:T(8,128)S(1)} %get-tuple-element.9.refs_1_, f32[8,1024]{1,0:T(8,128)S(1)} %get-tuple-element.10.refs_2_, ...), custom_call_target="tpu_custom_call" | custom-call | tf_op jit(solution)/shard_map/pallas_call | solution.py:625
